TPU v7x, 32 devices: a whole 2x2x4 slice. The times are simulated.
32 devices in a mesh: gx: 8 (over y, x, core), gy: 4 (over z).
Axes of the slice: x: 2, y: 2, z: 4, core: 2. Of those that a mesh axis runs over, the one named last changes fastest.
Arguments:
- objects: float32 [4, 4096, 2048], P(None, 'gx', 'gy'), may hold values from -3 to 3
- probe_wave: float32 [2, 256, 256], replicated, may hold values from -5 to 5
- prop_phase: float32 [256, 256], replicated, may hold values from -3.140625 to 3.140625
- intensity: float32 [128, 256, 256], P(('gx', 'gy')), may hold values from 0 to 1
- offsets: int32 [128, 2], P(('gx', 'gy')), may hold values from 0 to 512
- counts: int32 [32], P(('gx', 'gy')), may hold values from 1 to 4, 64 in all
Outputs:
- gradient: float32 [4, 4096, 2048], P(None, 'gx', 'gy')
Inputs may be any that keep to these rules, and one draw needn't show every extreme that they name: `counts`: every device has at least one live frame; the busiest has exactly 4.
All inputs are finite; a program needn't handle non-finite values.
Results may differ from a plain program's by a relative error of at most 0.00014.
Values sent between devices are 32-bit elements; how exact they have to be, the bound alone decides.
No kernel may reach another device: no remote copies, remote signals or barrier semaphores. Data moves between devices by JAX's collectives and lax.ppermute only.
A program may use at most 128 MiB of HBM per device.

v0:
```python
import math

import jax
import jax.numpy as jnp
from jax import lax
from jax.sharding import PartitionSpec as P

HIGH = lax.Precision.HIGHEST


def with_halo(cells, sides, width):
    for axis, dim in sides:
        count = lax.axis_size(axis)
        ends = count - 1
        head = lax.slice_in_dim(cells, 0, width, axis=dim)
        tail = lax.slice_in_dim(cells, cells.shape[dim] - width, cells.shape[dim], axis=dim)
        cells = jnp.concatenate(
            [
                lax.ppermute(tail, axis, [(i, (i + 1) % count) for i in range(ends)]),
                cells,
                lax.ppermute(head, axis, [((i + 1) % count, i) for i in range(ends)]),
            ],
            axis=dim,
        )
    return cells


def shifted(block, axis, distance):
    devices = range(lax.axis_size(axis))
    route = [(i - distance, i) for i in devices if i - distance in devices]
    return lax.ppermute(block, axis, route)


def product(left, right):
    return jnp.dot(left, right, precision=HIGH, preferred_element_type=jnp.float32)


def complex_product(left_re, left_im, right_re, right_im):
    return (
        product(left_re, right_re) - product(left_im, right_im),
        product(left_re, right_im) + product(left_im, right_re),
    )


def transform(real_part, imag_part, cosine, sine_part):
    upper_re, upper_im = complex_product(cosine, sine_part, real_part, imag_part)
    return complex_product(upper_re, upper_im, cosine, sine_part)


def times(left_re, left_im, right_re, right_im):
    return (left_re * right_re - left_im * right_im, left_re * right_im + left_im * right_re)


def conj_times(left_re, left_im, right_re, right_im):
    return (left_re * right_re + left_im * right_im, left_re * right_im - left_im * right_re)


def tables(frame_len, probe_wave, prop_phase):
    indices = jnp.arange(frame_len, dtype=jnp.int32)
    wrapped = indices[:, None] * indices[None, :] % frame_len
    angles = wrapped.astype(jnp.float32) * (2.0 * math.pi / frame_len)
    factor = 1.0 / math.sqrt(frame_len)
    cosine = jnp.cos(angles) * factor
    sine_part = jnp.sin(angles) * factor
    return (
        cosine,
        -sine_part,
        sine_part,
        probe_wave[0],
        probe_wave[1],
        jnp.cos(prop_phase),
        jnp.sin(prop_phase),
    )


def frame_gradient(window, measured, constants):
    cosine, forward_sine, inverse_sine, probe_re, probe_im, wave_re, wave_im = constants
    enter_re, enter_im = times(probe_re, probe_im, window[0], window[1])
    spec_re, spec_im = transform(enter_re, enter_im, cosine, forward_sine)
    spec_re, spec_im = times(wave_re, wave_im, spec_re, spec_im)
    carry_re, carry_im = transform(spec_re, spec_im, cosine, inverse_sine)
    exit_re, exit_im = times(carry_re, carry_im, window[2], window[3])
    far_re, far_im = transform(exit_re, exit_im, cosine, forward_sine)
    misfit = far_re * far_re + far_im * far_im - measured
    gexit_re, gexit_im = transform(misfit * far_re, misfit * far_im, cosine, inverse_sine)
    gtwo_re, gtwo_im = conj_times(carry_re, carry_im, gexit_re, gexit_im)
    gcarry_re, gcarry_im = conj_times(window[2], window[3], gexit_re, gexit_im)
    back_re, back_im = transform(gcarry_re, gcarry_im, cosine, forward_sine)
    back_re, back_im = conj_times(wave_re, wave_im, back_re, back_im)
    genter_re, genter_im = transform(back_re, back_im, cosine, inverse_sine)
    gone_re, gone_im = conj_times(probe_re, probe_im, genter_re, genter_im)
    return jnp.stack([gone_re, gone_im, gtwo_re, gtwo_im])


def shards(objects, probe_wave, prop_phase, intensity, offsets, counts):
    frame_len = intensity.shape[1]
    margin = frame_len // 2
    constants = tables(frame_len, probe_wave, prop_phase)
    padded = with_halo(objects, (("gx", 1), ("gy", 2)), margin)
    summed = jnp.zeros(padded.shape, jnp.float32)
    own_count = counts[0]
    anchor = jnp.int32(0)

    def window_at(source, row_start, col_start):
        return lax.dynamic_slice(source, (anchor, row_start, col_start), (4, frame_len, frame_len))

    def add_window(running, update, row_start, col_start):
        current = window_at(running, row_start, col_start)
        return lax.dynamic_update_slice(running, current + update, (anchor, row_start, col_start))

    def own_step(frame_slot, running):
        row_start = offsets[frame_slot, 0]
        col_start = offsets[frame_slot, 1]
        measured = lax.dynamic_index_in_dim(intensity, frame_slot, 0, keepdims=False)
        update = frame_gradient(window_at(padded, row_start, col_start), measured, constants)
        return add_window(running, update, row_start, col_start)

    summed = lax.fori_loop(0, own_count, own_step, summed)
    from_below = shifted(summed[:, :margin, :], "gx", -1)
    from_above = shifted(summed[:, -margin:, :], "gx", 1)
    inner = summed[:, margin:-margin, :]
    inner = inner.at[:, :margin, :].add(from_above).at[:, -margin:, :].add(from_below)
    from_right = shifted(inner[:, :, :margin], "gy", -1)
    from_left = shifted(inner[:, :, -margin:], "gy", 1)
    folded = inner[:, :, margin:-margin]
    folded = folded.at[:, :, :margin].add(from_left).at[:, :, -margin:].add(from_right)
    return folded


def solution(mesh):
    return jax.shard_map(
        shards,
        mesh=mesh,
        in_specs=(
            P(None, "gx", "gy"),
            P(),
            P(),
            P(("gx", "gy"), None, None),
            P(("gx", "gy"), None),
            P(("gx", "gy")),
        ),
        out_specs=P(None, "gx", "gy"),
        check_vma=False,
    )
```

profile of v0, /device:TPU:11, one launch (start us, length us, event | category | flops | bytes accessed | tf_op | source)
XLA Modules:
  0.0 554.9 jit_solution(1288340216803666110)
XLA Ops:
  0.0 1.9 fusion.297
  1.9 3.7 collective-permute-start
  5.6 1.9 collective-permute-start.1
  7.5 18.3 %collective-permute-done = f32[4,128,512]{2,1,0:T(8,128)S(1)} collective-permute-done((f32[4,128,512]{2,1,0:T(8,128)S(1)}, f32[4,128,512]{2,1,0:T(8,128)S(1)}, u32[]{:S(2)}, u32[]{:S(2)}) %collective-permute-start) | collective-permute-done | bytes 1048608 | tf_op jit(solution)/shard_map/ppermute | solution.py:19
  26.4 3.8 collective-permute-done.1
  30.3 2.6 copy-done
  33.0 1.9 fusion.296
  34.9 3.2 collective-permute-start.2
  38.1 2.2 collective-permute-start.3
  41.3 31.4 %collective-permute-done.2 = f32[4,768,128]{2,1,0:T(8,128)S(1)} collective-permute-done((f32[4,768,128]{2,1,0:T(8,128)}, f32[4,768,128]{2,1,0:T(8,128)S(1)}, u32[]{:S(2)}, u32[]{:S(2)}) %collective-permute-start.2) | collective-permute-done | bytes 1572896 | tf_op jit(solution)/shard_map/ppermute | solution.py:19
  72.7 3.2 collective-permute-done.3
  75.9 7.7 %pad_maximum_fusion = f32[4,768,768]{2,1,0:T(8,128)} fusion(f32[4,768,128]{2,1,0:T(8,128)} %collective-permute-done.3, f32[4,768,512]{2,1,0:T(8,128)} %copy-done, f32[4,768,128]{2,1,0:T(8,128)S(1)} %collective-permute-done.2), kind=kLoop, calls=%fused_computation.327 | loop fusion | flops 4718592 | bytes 18874368 | tf_op jit(solution)/shard_map/concatenate | solution.py:17
  83.6 4.4 broadcast_in_dim.2
  88.1 101.7 %while.16 = (s32[]{:T(128)}, f32[4,768,768]{2,1,0:T(8,128)}, s32[]{:T(128)}, s32[4,2]{0,1:T(2,128)S(1)}, f32[4,768,768]{2,1,0:T(8,128)}, /*index=5*/f32[256,256]...) while((s32[]{:T(128)}, f32[4,768,768]{2,1,0:T(8,128)}, ...), condition=%wide.region_1.2_spmd.clone.clone, body=%wide.region_0.1_spmd.clone.clone.sunk | while | flops 9717415936 | bytes 45613436 | solution.py:118
  105.4 2.1 multiply_add_fusion.9
  117.9 2.8 multiply_add_fusion.10
  131.1 2.7 fusion.500
  144.2 3.1 multiply_subtract_fusion.7
  157.6 1.7 multiply_subtract_fusion.8
  171.1 1.8 maximum_add_fusion.2
  173.0 12.3 %dynamic_update_slice.6 = f32[4,768,768]{2,1,0:T(8,128)} dynamic-update-slice(f32[4,768,768]{2,1,0:T(8,128)} %get-tuple-element.532, f32[4,256,256]{2,1,0:T(8,128)S(1)} %maximum_add_fusion.2, s32[]{:T(128)} %constant.132.clone.1..sunk, s32[]{:T(128)S(6)} %select_n.307, s32[]{:T(128)S(6)} %select_n.308) | dynamic-update-slice | bytes 2097156 | tf_op jit(solution)/shard_map/while/body/dynamic_update_slice | solution.py:109
  191.3 1.9 collective-permute-start.4
  193.2 3.3 slice.154
  196.5 193.1 %collective-permute-done.4 = f32[4,128,768]{2,1,0:T(8,128)S(1)} collective-permute-done((f32[4,128,768]{2,1,0:T(8,128)S(1)}, f32[4,128,768]{2,1,0:T(8,128)S(1)}, u32[]{:S(2)}, u32[]{:S(2)}) %collective-permute-start.4) | collective-permute-done | bytes 1572896 | tf_op jit(solution)/shard_map/ppermute | solution.py:31
  389.7 2.3 fusion.294
  392.0 18.8 %collective-permute-start.5 = (f32[4,128,768]{2,1,0:T(8,128)S(1)}, f32[4,128,768]{2,1,0:T(8,128)S(1)}, u32[]{:S(2)}, u32[]{:S(2)}) collective-permute-start(f32[4,128,768]{2,1,0:T(8,128)S(1)} %get-tuple-element.402), channel_id=1, source_target_pairs={{4,0},{8,4},{12,8},{16,12},{20,16},{24,20},{28,24},{5,1},{9,5},{13... | collective-permute-start | bytes 4718600 | tf_op jit(solution)/shard_map/ppermute | solution.py:31
  410.8 3.8 collective-permute-done.5
  415.1 80.7 %collective-permute-start.6 = (f32[4,512,128]{2,1,0:T(8,128)S(1)}, f32[4,512,128]{2,1,0:T(8,128)S(1)}, u32[]{:S(2)}, u32[]{:S(2)}) collective-permute-start(f32[4,512,128]{2,1,0:T(8,128)S(1)} %get-tuple-element.405), channel_id=1, source_target_pairs={{0,1},{1,2},{2,3},{4,5},{5,6},{6,7},{8,9},{9,10},{10,11},{12,13},{... | collective-permute-start | bytes 3145736 | tf_op jit(solution)/shard_map/ppermute | solution.py:31
  495.8 20.3 %collective-permute-start.7 = (f32[4,512,128]{2,1,0:T(8,128)S(1)}, f32[4,512,128]{2,1,0:T(8,128)S(1)}, u32[]{:S(2)}, u32[]{:S(2)}) collective-permute-start(f32[4,512,128]{2,1,0:T(8,128)S(1)} %get-tuple-element.404), channel_id=1, source_target_pairs={{1,0},{2,1},{3,2},{5,4},{6,5},{7,6},{9,8},{10,9},{11,10},{13,12},{... | collective-permute-start | bytes 3145736 | tf_op jit(solution)/shard_map/ppermute | solution.py:31
  516.6 9.9 %collective-permute-done.6 = f32[4,512,128]{2,1,0:T(8,128)S(1)} collective-permute-done((f32[4,512,128]{2,1,0:T(8,128)S(1)}, f32[4,512,128]{2,1,0:T(8,128)S(1)}, u32[]{:S(2)}, u32[]{:S(2)}) %collective-permute-start.6) | collective-permute-done | bytes 1048608 | tf_op jit(solution)/shard_map/ppermute | solution.py:31
  526.8 25.6 %collective-permute-done.7 = f32[4,512,128]{2,1,0:T(8,128)S(1)} collective-permute-done((f32[4,512,128]{2,1,0:T(8,128)S(1)}, f32[4,512,128]{2,1,0:T(8,128)S(1)}, u32[]{:S(2)}, u32[]{:S(2)}) %collective-permute-start.7) | collective-permute-done | bytes 1048608 | tf_op jit(solution)/shard_map/ppermute | solution.py:31
  552.3 2.3 fusion.292
  (66 shorter events, 69.6 us)
Async XLA Ops:
  0.0 25.9 %copy-start.1 = (f32[4,512,512]{2,1,0:T(8,128)S(1)}, f32[4,512,512]{2,1,0:T(8,128)}, u32[]{:S(2)}) copy-start(f32[4,512,512]{2,1,0:T(8,128)} %param.16) | copy-start | bytes 12582916
  1.9 23.9 %collective-permute-start = (f32[4,128,512]{2,1,0:T(8,128)S(1)}, f32[4,128,512]{2,1,0:T(8,128)S(1)}, u32[]{:S(2)}, u32[]{:S(2)}) collective-permute-start(f32[4,128,512]{2,1,0:T(8,128)S(1)} %get-tuple-element.409), channel_id=1, source_target_pairs={{0,4},{4,8},{8,12},{12,16},{16,20},{20,24},{24,28},{1,5},{5,9},{9,... | collective-permute-start | bytes 3145736 | tf_op jit(solution)/shard_map/ppermute | solution.py:19
  5.6 24.6 %collective-permute-start.1 = (f32[4,128,512]{2,1,0:T(8,128)S(1)}, f32[4,128,512]{2,1,0:T(8,128)S(1)}, u32[]{:S(2)}, u32[]{:S(2)}) collective-permute-start(f32[4,128,512]{2,1,0:T(8,128)S(1)} %get-tuple-element.408), channel_id=1, source_target_pairs={{4,0},{8,4},{12,8},{16,12},{20,16},{24,20},{28,24},{5,1},{9,5},{13... | collective-permute-start | bytes 3145736 | tf_op jit(solution)/shard_map/ppermute | solution.py:21
  26.4 13.9 %copy-start.3 = (f32[2,256,256]{2,1,0:T(8,128)S(1)}, f32[2,256,256]{2,1,0:T(8,128)}, u32[]{:S(2)}) copy-start(f32[2,256,256]{2,1,0:T(8,128)} %param.17) | copy-start | bytes 1572868
  26.4 14.0 %copy-start.4 = (f32[256,256]{1,0:T(8,128)S(1)}, f32[256,256]{1,0:T(8,128)}, u32[]{:S(2)}) copy-start(f32[256,256]{1,0:T(8,128)} %param.18) | copy-start | bytes 786436
  30.3 2.7 copy-start
  34.9 37.8 %collective-permute-start.2 = (f32[4,768,128]{2,1,0:T(8,128)}, f32[4,768,128]{2,1,0:T(8,128)S(1)}, u32[]{:S(2)}, u32[]{:S(2)}) collective-permute-start(f32[4,768,128]{2,1,0:T(8,128)} %get-tuple-element.406), channel_id=1, source_target_pairs={{0,1},{1,2},{2,3},{4,5},{5,6},{6,7},{8,9},{9,10},{10,11},{12,13},{... | collective-permute-start | bytes 4718600 | tf_op jit(solution)/shard_map/ppermute | solution.py:19
  38.1 37.8 %collective-permute-start.3 = (f32[4,768,128]{2,1,0:T(8,128)}, f32[4,768,128]{2,1,0:T(8,128)}, u32[]{:S(2)}, u32[]{:S(2)}) collective-permute-start(f32[4,768,128]{2,1,0:T(8,128)} %get-tuple-element.407), channel_id=1, source_target_pairs={{1,0},{2,1},{3,2},{5,4},{6,5},{7,6},{9,8},{10,9},{11,10},{13,12},{... | collective-permute-start | bytes 4718600 | tf_op jit(solution)/shard_map/ppermute | solution.py:21
  83.6 4.4 copy-start.5
  191.3 198.4 %collective-permute-start.4 = (f32[4,128,768]{2,1,0:T(8,128)S(1)}, f32[4,128,768]{2,1,0:T(8,128)S(1)}, u32[]{:S(2)}, u32[]{:S(2)}) collective-permute-start(f32[4,128,768]{2,1,0:T(8,128)S(1)} %slice.156), channel_id=1, source_target_pairs={{0,4},{4,8},{8,12},{12,16},{16,20},{20,24},{24,28},{1,5},{5,9},{9,... | collective-permute-start | bytes 4718600 | tf_op jit(solution)/shard_map/ppermute | solution.py:31
  392.0 22.6 %collective-permute-start.5 = (f32[4,128,768]{2,1,0:T(8,128)S(1)}, f32[4,128,768]{2,1,0:T(8,128)S(1)}, u32[]{:S(2)}, u32[]{:S(2)}) collective-permute-start(f32[4,128,768]{2,1,0:T(8,128)S(1)} %get-tuple-element.402), channel_id=1, source_target_pairs={{4,0},{8,4},{12,8},{16,12},{20,16},{24,20},{28,24},{5,1},{9,5},{13... | collective-permute-start | bytes 4718600 | tf_op jit(solution)/shard_map/ppermute | solution.py:31
  415.1 111.4 %collective-permute-start.6 = (f32[4,512,128]{2,1,0:T(8,128)S(1)}, f32[4,512,128]{2,1,0:T(8,128)S(1)}, u32[]{:S(2)}, u32[]{:S(2)}) collective-permute-start(f32[4,512,128]{2,1,0:T(8,128)S(1)} %get-tuple-element.405), channel_id=1, source_target_pairs={{0,1},{1,2},{2,3},{4,5},{5,6},{6,7},{8,9},{9,10},{10,11},{12,13},{... | collective-permute-start | bytes 3145736 | tf_op jit(solution)/shard_map/ppermute | solution.py:31
  495.8 56.5 %collective-permute-start.7 = (f32[4,512,128]{2,1,0:T(8,128)S(1)}, f32[4,512,128]{2,1,0:T(8,128)S(1)}, u32[]{:S(2)}, u32[]{:S(2)}) collective-permute-start(f32[4,512,128]{2,1,0:T(8,128)S(1)} %get-tuple-element.404), channel_id=1, source_target_pairs={{1,0},{2,1},{3,2},{5,4},{6,5},{7,6},{9,8},{10,9},{11,10},{13,12},{... | collective-permute-start | bytes 3145736 | tf_op jit(solution)/shard_map/ppermute | solution.py:31
  526.7 25.6 %copy-start.2 = (f32[4,512,512]{2,1,0:T(8,128)}, f32[4,512,512]{2,1,0:T(8,128)S(1)}, u32[]{:S(2)}) copy-start(f32[4,512,512]{2,1,0:T(8,128)S(1)} %fusion.293) | copy-start | bytes 12582916
where the time goes:
time: 560 us; the launch traced here: 555 us
  waiting for transfers between devices  289 us (52%)
  starting transfers between devices  133 us (24%)
  matrix products  75.7 us (14%)
  local copies, waits for them, and re-layouts  31.1 us (6%)
  other arithmetic  16 us (3%)
  loops' own time  9.78 us (2%)
    ppermute x4, waiting for transfers between devices, shifted(): return lax.ppermute(block, axis, route)  232 us
    ppermute x4, starting transfers between devices, shifted(): return lax.ppermute(block, axis, route)  122 us
    dot_general x48, matrix products, product(): jnp.dot(left, right, precision=HIGH, preferred_element_type=jnp.float32)  75.7 us
    ppermute x2, waiting for transfers between devices, with_halo(): lax.ppermute(tail, axis, [(i, (i + 1) % count) for i in range(ends)])  49.7 us
    dynamic_update_slice x1, local copies, waits for them, and re-layouts, add_window(): lax.dynamic_update_slice(running, current + update, (anchor, row_start, c...  12.3 us
  transfers between devices with their start and end apart: 8, of which 8 were waited for; matrix products, arithmetic and copies ran while one was open for 1% of the time, Pallas kernels for 0%

commit v1 on v0

v1 whole, which is shorter than its diff:
```python
import math

import jax
import jax.numpy as jnp
import numpy as np
from jax import lax
from jax.experimental import pallas as pl
from jax.experimental.pallas import tpu as pltpu
from jax.sharding import PartitionSpec as P


ROWS = 32


def half_tables(frame):
    half = frame // 2
    n = np.arange(half)
    angle = 2.0 * np.pi * ((n[:, None] * n[None, :]) % half) / half
    scale = 1.0 / math.sqrt(frame)
    c, s = np.cos(angle) * scale, np.sin(angle) * scale
    right = np.block([[c, -s], [s, c]])
    turn = 2.0 * np.pi * n / frame
    return right, np.cos(turn), np.sin(turn)


def split_const(m):
    hi = m.astype(np.float32).astype(jnp.bfloat16)
    lo = (m - hi.astype(np.float64)).astype(np.float32).astype(jnp.bfloat16)
    return hi, lo


def put(hi_ref, lo_ref, rows, cols, value):
    hi = value.astype(jnp.bfloat16)
    hi_ref[rows, cols] = hi
    lo_ref[rows, cols] = (value - hi.astype(jnp.float32)).astype(jnp.bfloat16)


def mm(left, right):
    return jnp.dot(left, right, preferred_element_type=jnp.float32)


def cmul(ar, ai, br, bi):
    return ar * br - ai * bi, ar * bi + ai * br


def cmul_conj(ar, ai, br, bi):
    return ar * br + ai * bi, ar * bi - ai * br


def frame_kernel(
    scal, tile, left, right, over, lcor, rcor, ext_e, inten, probe, prop, mats, twl, twc,
    g_tile, g_left, g_right, g_over, g_ext, g_ol, g_or, g_el, g_er,
    obj, acc, win, car, fld, lh, ll, rh, rl, dd, sems,
):
    frame = probe.shape[1]
    half = frame // 2
    size = tile.shape[1]
    ntile = size // half
    even = scal[1] == 0
    e_row = jnp.where(even, half + size, 0)
    o_row = jnp.where(even, 0, half + size)
    e_row = pl.multiple_of(e_row, half)
    o_row = pl.multiple_of(o_row, half)
    mid = pl.ds(half, size)

    def blocks(array, width):
        return [array.at[:, :, pl.ds(half * j, half)] for j in range(width)]

    def moves(big, t, l, r, o, ol, orr, e, el, er):
        pairs = [
            (l, big.at[:, 0, mid, :]),
            (r, big.at[:, ntile + 1, mid, :]),
            (ol, big.at[:, 0, pl.ds(o_row, half), :]),
            (orr, big.at[:, ntile + 1, pl.ds(o_row, half), :]),
            (el, big.at[:, 0, pl.ds(e_row, half), :]),
            (er, big.at[:, ntile + 1, pl.ds(e_row, half), :]),
        ]
        for j in range(ntile):
            pairs.append((o[j], big.at[:, j + 1, pl.ds(o_row, half), :]))
            pairs.append((e[j], big.at[:, j + 1, pl.ds(e_row, half), :]))
            pairs.append((t[j], big.at[:, j + 1, mid, :]))
        return pairs

    strip = blocks(ext_e, ntile + 2)
    loads = [
        pltpu.make_async_copy(src, dst, sems.at[i])
        for i, (src, dst) in enumerate(
            moves(
                obj, blocks(tile, ntile), left, right, blocks(over, ntile), lcor, rcor,
                strip[1:-1], strip[0], strip[-1],
            )
        )
    ]
    for copy in loads:
        copy.start()

    def clear(i, carry):
        acc[i // (ntile + 2), i % (ntile + 2)] = jnp.zeros(acc.shape[2:], jnp.float32)
        return carry

    lax.fori_loop(0, acc.shape[0] * (ntile + 2), clear, 0)
    for copy in loads:
        copy.wait()

    lane = lax.broadcasted_iota(jnp.int32, (ROWS, half), 1)
    low, high = slice(0, half), slice(half, frame)

    def right_forward(source):
        for rb in range(0, frame, ROWS):
            rows = slice(rb, rb + ROWS)
            xr, xi = source(rows)
            ar, br, ai, bi = xr[:, :half], xr[:, half:], xi[:, :half], xi[:, half:]
            put(lh, ll, rows, low, ar + br)
            put(lh, ll, rows, high, ai + bi)
            dr, di = ar - br, ai - bi
            c, s = twl[0:1, :], twl[1:2, :]
            vrows = slice(frame + rb, frame + rb + ROWS)
            put(lh, ll, vrows, low, dr * c + di * s)
            put(lh, ll, vrows, high, di * c - dr * s)
        dd[...] = mm(lh[...], mats[0]) + mm(ll[...], mats[0]) + mm(lh[...], mats[1])

    def left_forward():
        for q in range(2):
            for rb in range(0, half, ROWS):
                rows = slice(rb, rb + ROWS)
                t = pl.ds(q * frame + rb, ROWS)
                b = pl.ds(q * frame + half + rb, ROWS)
                ar, ai, br, bi = dd[t, low], dd[t, high], dd[b, low], dd[b, high]
                irows = slice(half + rb, half + rb + ROWS)
                ucols = slice(q * half, (q + 1) * half)
                vcols = slice(frame + q * half, frame + (q + 1) * half)
                put(rh, rl, rows, ucols, ar + br)
                put(rh, rl, irows, ucols, ai + bi)
                dr, di = ar - br, ai - bi
                c, s = twc[0, rows, :], twc[1, rows, :]
                put(rh, rl, rows, vcols, dr * c + di * s)
                put(rh, rl, irows, vcols, di * c - dr * s)
        return mm(mats[2], rh[...]) + mm(mats[2], rl[...]) + mm(mats[3], rh[...])

    def forward(source):
        right_forward(source)
        fld[...] = left_forward()

    def inverse(source, sink):
        for rb in range(0, half, ROWS):
            rows = slice(rb, rb + ROWS)
            xr, xi = source(rows)
            put(rh, rl, rows, slice(None), xr)
            put(rh, rl, slice(half + rb, half + rb + ROWS), slice(None), xi)
        fld[...] = mm(mats[0], rh[...]) + mm(mats[0], rl[...]) + mm(mats[1], rh[...])
        for q in range(2):
            for rb in range(0, half, ROWS):
                rows = slice(rb, rb + ROWS)
                irows = slice(half + rb, half + rb + ROWS)
                ecols = slice(q * half, (q + 1) * half)
                ocols = slice(frame + q * half, frame + (q + 1) * half)
                er, ei, wr, wi = fld[rows, ecols], fld[irows, ecols], fld[rows, ocols], fld[irows, ocols]
                c, s = twc[0, rows, :], twc[1, rows, :]
                tr, ti = wr * c - wi * s, wi * c + wr * s
                top = slice(q * frame + rb, q * frame + rb + ROWS)
                bot = slice(q * frame + half + rb, q * frame + half + rb + ROWS)
                put(lh, ll, top, low, er + tr)
                put(lh, ll, top, high, ei + ti)
                put(lh, ll, bot, low, er - tr)
                put(lh, ll, bot, high, ei - ti)
        dd[...] = mm(lh[...], mats[2]) + mm(ll[...], mats[2]) + mm(lh[...], mats[3])
        for rb in range(0, frame, ROWS):
            rows = slice(rb, rb + ROWS)
            orows = slice(frame + rb, frame + rb + ROWS)
            er, ei, wr, wi = dd[rows, low], dd[rows, high], dd[orows, low], dd[orows, high]
            c, s = twl[0:1, :], twl[1:2, :]
            tr, ti = wr * c - wi * s, wi * c + wr * s
            sink(rows, er + tr, ei + ti, er - tr, ei - ti)

    def step(f, carry):
        r = scal[2 + 2 * f]
        c = scal[3 + 2 * f]
        j = jnp.minimum(c // half, ntile - 1)
        cs = c - j * half
        back = lax.rem(half - cs, half)
        fore = lax.rem(cs, half)
        keep = lane + cs < half
        spill = lane >= cs

        for k in range(4):
            for rb in range(0, frame, ROWS):
                parts = [
                    pltpu.roll(obj[k, j + t, pl.ds(r + rb, ROWS), :], back, 1) for t in range(3)
                ]
                win[k, rb:rb + ROWS, low] = jnp.where(keep, parts[0], parts[1])
                win[k, rb:rb + ROWS, high] = jnp.where(keep, parts[1], parts[2])

        def place(k, rows, first, second):
            a, b = pltpu.roll(first, fore, 1), pltpu.roll(second, fore, 1)
            at = pl.ds(r + rows.start, ROWS)
            zero = jnp.zeros_like(a)
            acc[k, j, at, :] += jnp.where(spill, a, zero)
            acc[k, j + 1, at, :] += jnp.where(spill, b, a)
            acc[k, j + 2, at, :] += jnp.where(spill, zero, b)

        def enter(rows):
            return cmul(probe[0, rows, :], probe[1, rows, :], win[0, rows, :], win[1, rows, :])

        def lower(rows):
            return slice(half + rows.start, half + rows.stop)

        def propagate(rows):
            return cmul(prop[0, rows, :], prop[1, rows, :], fld[rows, :], fld[lower(rows), :])

        def propagate_back(rows):
            return cmul_conj(prop[0, rows, :], prop[1, rows, :], fld[rows, :], fld[lower(rows), :])

        def carried(rows, ar, ai, br, bi):
            car[0, rows, low] = ar
            car[1, rows, low] = ai
            car[0, rows, high] = br
            car[1, rows, high] = bi

        def exit_wave(rows):
            return cmul(car[0, rows, :], car[1, rows, :], win[2, rows, :], win[3, rows, :])

        def misfit(rows):
            fr, fi = fld[rows, :], fld[lower(rows), :]
            m = fr * fr + fi * fi - inten[f, rows, :]
            return m * fr, m * fi

        def grad_exit(rows, ar, ai, br, bi):
            lr, li = cmul_conj(car[0, rows, low], car[1, rows, low], ar, ai)
            hr, hi = cmul_conj(car[0, rows, high], car[1, rows, high], br, bi)
            place(2, rows, lr, hr)
            place(3, rows, li, hi)
            for cols, (gr, gi) in ((low, (ar, ai)), (high, (br, bi))):
                xr, xi = cmul_conj(win[2, rows, cols], win[3, rows, cols], gr, gi)
                win[0, rows, cols] = xr
                win[1, rows, cols] = xi

        def grad_enter(rows, ar, ai, br, bi):
            lr, li = cmul_conj(probe[0, rows, low], probe[1, rows, low], ar, ai)
            hr, hi = cmul_conj(probe[0, rows, high], probe[1, rows, high], br, bi)
            place(0, rows, lr, hr)
            place(1, rows, li, hi)

        forward(enter)
        inverse(propagate, carried)
        forward(exit_wave)
        inverse(misfit, grad_exit)
        forward(lambda rows: (win[0, rows, :], win[1, rows, :]))
        inverse(propagate_back, grad_enter)
        return carry

    lax.fori_loop(0, scal[0], step, 0)

    stores = [
        pltpu.make_async_copy(src, dst, sems.at[i])
        for i, (dst, src) in enumerate(
            moves(
                acc, blocks(g_tile, ntile), g_left, g_right, blocks(g_over, ntile), g_ol, g_or,
                blocks(g_ext, ntile), g_el, g_er,
            )
        )
    ]
    for copy in stores:
        copy.start()
    for copy in stores:
        copy.wait()


def run_frames(scal, pieces, inten, probe, prop, frame):
    right, tc, ts = half_tables(frame)
    half = frame // 2
    rhi, rlo = split_const(right)
    mats = np.stack([rhi, rlo, np.ascontiguousarray(rhi.T), np.ascontiguousarray(rlo.T)])
    twl = np.zeros((8, half), np.float32)
    twl[0], twl[1] = tc, ts
    twc = np.stack([np.repeat(tc[:, None], half, 1), np.repeat(ts[:, None], half, 1)]).astype(np.float32)
    channels, size, _ = pieces[0].shape
    ntile = size // half
    hbm = pl.BlockSpec(memory_space=pl.ANY)
    vmem = pl.BlockSpec(memory_space=pltpu.VMEM)
    big = (channels, ntile + 2, size + frame, half)
    tile, left, right, over, lcor, rcor, _ = pieces
    outs = [
        jax.ShapeDtypeStruct(p.shape, jnp.float32)
        for p in (tile, left, right, over, over, lcor, rcor, lcor, rcor)
    ]
    copies = 3 * ntile + 6
    return pl.pallas_call(
        frame_kernel,
        out_shape=outs,
        in_specs=[pl.BlockSpec(memory_space=pltpu.SMEM)] + [hbm] * len(pieces) + [vmem] * 6,
        out_specs=[hbm] * len(outs),
        scratch_shapes=[
            pltpu.VMEM(big, jnp.float32),
            pltpu.VMEM(big, jnp.float32),
            pltpu.VMEM((4, frame, frame), jnp.float32),
            pltpu.VMEM((2, frame, frame), jnp.float32),
            pltpu.VMEM((frame, 2 * frame), jnp.float32),
            pltpu.VMEM((2 * frame, frame), jnp.bfloat16),
            pltpu.VMEM((2 * frame, frame), jnp.bfloat16),
            pltpu.VMEM((frame, 2 * frame), jnp.bfloat16),
            pltpu.VMEM((frame, 2 * frame), jnp.bfloat16),
            pltpu.VMEM((2 * frame, frame), jnp.float32),
            pltpu.SemaphoreType.DMA((copies,)),
        ],
        compiler_params=pltpu.CompilerParams(vmem_limit_bytes=40 * 1024 * 1024),
        cost_estimate=pl.CostEstimate(flops=40_000_000_000, bytes_accessed=30_000_000, transcendentals=0),
        name="frames",
    )(scal, *pieces, inten, probe, prop, mats, twl, twc)


def parity_kernel(inten, prop, pick, inten_out, prop_out, mid):
    half = pick.shape[0] // 2

    def sort(src, dst, index):
        x = src[index]
        top = x.astype(jnp.bfloat16)
        rest = x - top.astype(jnp.float32)
        middle = rest.astype(jnp.bfloat16)
        last = (rest - middle.astype(jnp.float32)).astype(jnp.bfloat16)
        out = mm(top, pick[...]) + mm(middle, pick[...]) + mm(last, pick[...])
        mid[2 * index] = out[:, :half]
        mid[2 * index + 1] = out[:, half:]
        for q in range(2):
            for p in range(2):
                cols = slice((2 * q + p) * half, (2 * q + p + 1) * half)
                dst[index, :, cols] = mid[2 * index + p, pl.ds(q, half, stride=2), :]

    for i in range(inten.shape[0]):
        sort(inten, inten_out, i)
    for i in range(prop.shape[0]):
        sort(prop, prop_out, i)


def by_parity(inten, prop):
    frame = inten.shape[-1]
    half = frame // 2
    pick = np.zeros((frame, frame), np.float32)
    n = np.arange(half)
    pick[2 * n, n] = 1.0
    pick[2 * n + 1, half + n] = 1.0
    vmem = pl.BlockSpec(memory_space=pltpu.VMEM)
    return pl.pallas_call(
        parity_kernel,
        out_shape=[
            jax.ShapeDtypeStruct((x.shape[0], half, 2 * frame), jnp.float32) for x in (inten, prop)
        ],
        in_specs=[vmem] * 3,
        out_specs=[vmem] * 2,
        scratch_shapes=[pltpu.VMEM((2 * inten.shape[0], frame, half), jnp.float32)],
        cost_estimate=pl.CostEstimate(flops=4_000_000_000, bytes_accessed=3_000_000, transcendentals=0),
        name="parity",
    )(inten, prop, pick.astype(jnp.bfloat16))


def pair_route(count, first):
    route = []
    for i in range(first, count - 1, 2):
        route += [(i, i + 1), (i + 1, i)]
    return route


def shards(objects, probe_wave, prop_phase, intensity, offsets, counts):
    frame = intensity.shape[1]
    margin = frame // 2
    size_r, size_c = objects.shape[1:]
    nx, ny = lax.axis_size("gx"), lax.axis_size("gy")
    parity = lax.axis_index("gx") % 2
    to_left = [(i, i - 1) for i in range(1, ny)]
    to_right = [(i, i + 1) for i in range(ny - 1)]
    e_route, o_route = pair_route(nx, 0), pair_route(nx, 1)
    e_start = jnp.where(parity == 0, size_r - margin, 0)
    o_start = jnp.where(parity == 0, 0, size_r - margin)

    def band(x, start):
        return lax.dynamic_slice_in_dim(x, start, margin, 1)

    def corner(x_route, y_route):
        return [(a * ny + c, b * ny + d) for a, b in x_route for c, d in y_route]

    def add_at(x, row, col, update):
        at = (0, row, col)
        old = lax.dynamic_slice(x, at, update.shape)
        return lax.dynamic_update_slice(x, old + update, at)

    over = lax.ppermute(band(objects, o_start), "gx", o_route)
    right = lax.ppermute(objects[:, :, :margin], "gy", to_left)
    left = lax.ppermute(objects[:, :, -margin:], "gy", to_right)
    first, last = over[:, :, :margin], over[:, :, -margin:]
    rcor = lax.ppermute(first, "gy", to_left)
    lcor = lax.ppermute(last, "gy", to_right)
    strip = jnp.concatenate([band(left, e_start), band(objects, e_start), band(right, e_start)], axis=2)
    ext = lax.ppermute(strip, "gx", e_route)

    waves = jnp.stack([jnp.cos(prop_phase), jnp.sin(prop_phase)])
    inten, waves = by_parity(intensity, waves)
    scal = jnp.concatenate([counts, parity[None].astype(jnp.int32), offsets.reshape(-1)])
    pieces = [objects, left, right, over, lcor, rcor, ext]
    tile, left, right, over, ext, ol, orr, el, er = run_frames(
        scal, pieces, inten, probe_wave, waves, frame
    )

    both = ("gx", "gy")
    from_right = lax.ppermute(left, "gy", to_left)
    from_left = lax.ppermute(right, "gy", to_right)
    over = lax.ppermute(over, "gx", o_route)
    ext = lax.ppermute(ext, "gx", e_route)
    ol = lax.ppermute(ol, both, corner(o_route, to_left))
    orr = lax.ppermute(orr, both, corner(o_route, to_right))
    el = lax.ppermute(el, both, corner(e_route, to_left))
    er = lax.ppermute(er, both, corner(e_route, to_right))
    far = size_c - margin
    tile = add_at(tile, e_start, 0, ext)
    tile = add_at(tile, o_start, 0, over)
    tile = add_at(tile, 0, far, from_right)
    tile = add_at(tile, 0, 0, from_left)
    tile = add_at(tile, o_start, far, ol)
    tile = add_at(tile, o_start, 0, orr)
    tile = add_at(tile, e_start, far, el)
    return add_at(tile, e_start, 0, er)


def solution(mesh):
    return jax.shard_map(
        shards,
        mesh=mesh,
        in_specs=(
            P(None, "gx", "gy"),
            P(),
            P(),
            P(("gx", "gy"), None, None),
            P(("gx", "gy"), None),
            P(("gx", "gy")),
        ),
        out_specs=P(None, "gx", "gy"),
        check_vma=False,
    )
```

time: 560 us -> 135 us (0.24)
  waiting for transfers between devices: 289 us -> 26.7 us
  matrix products: 75.7 us -> 0 us
  starting transfers between devices: 133 us -> 58.6 us
  local copies, waits for them, and re-layouts: 31.1 us -> 12.2 us
  Pallas kernels: 0 us -> 15.9 us
  loops' own time: 9.78 us -> 0 us
    ppermute x8 -> x14, waiting for transfers between devices: 289 us -> 26.7 us  [the longest x1 13.8 us: shards(): right = lax.ppermute(objects[:, :, :margin], 'gy', to_left)]
    dot_general x48 -> x0, matrix products: 75.7 us -> none  [product(): jnp.dot(left, right, precision=HIGH, preferred_element_type=jnp.float32)]
    ppermute x8 -> x14, starting transfers between devices: 133 us -> 58.6 us  [the longest x1 12.9 us: shards(): ext = lax.ppermute(ext, 'gx', e_route)]
    dynamic_update_slice x0 -> x8, other arithmetic: none -> 16.2 us  [add_at(): return lax.dynamic_update_slice(x, old + update, at)]
    pallas_call x0 -> x2, Pallas kernels: none -> 15.9 us  [the longest x1 12.7 us: run_frames(): pl.pallas_call(frame_kernel, out_shape=outs, in_specs=[pl.BlockSpec(memor...]
    dynamic_update_slice x1 -> x0, local copies, waits for them, and re-layouts: 12.3 us -> none  [add_window(): lax.dynamic_update_slice(running, current + update, (anchor, row_start, c...]
    another operation x1 -> x0, loops' own time: 9.78 us -> none  [shards(): summed = lax.fori_loop(0, own_count, own_step, summed)]
    concatenate x1 -> x2, other arithmetic: 7.74 us -> 1.33 us  [the longest x1 1.25 us: shards(): jnp.concatenate([band(left, e_start), band(objects, e_start), band(right,...]
  transfers between devices with their start and end apart: 8 -> 14, of which waited for: 8 -> 6; matrix products, arithmetic and copies ran while one was open for 1% -> 16% of each run, Pallas kernels for 0% -> 2%
where the time goes in v1:
time: 135 us; the launch traced here: 133 us
  starting transfers between devices  58.6 us (43%)
  waiting for transfers between devices  26.7 us (20%)
  other arithmetic  18.3 us (14%)
  Pallas kernels  15.9 us (12%)
  local copies, waits for them, and re-layouts  12.2 us (9%)
    dynamic_update_slice x8, other arithmetic, add_at(): return lax.dynamic_update_slice(x, old + update, at)  16.2 us
    ppermute x1, waiting for transfers between devices, shards(): right = lax.ppermute(objects[:, :, :margin], 'gy', to_left)  13.8 us
    ppermute x1, starting transfers between devices, shards(): ext = lax.ppermute(ext, 'gx', e_route)  12.9 us
    pallas_call x1, Pallas kernels, run_frames(): pl.pallas_call(frame_kernel, out_shape=outs, in_specs=[pl.BlockSpec(memor...  12.7 us
    ppermute x1, starting transfers between devices, shards(): from_right = lax.ppermute(left, 'gy', to_left)  7.83 us
    ppermute x1, starting transfers between devices, shards(): ol = lax.ppermute(ol, both, corner(o_route, to_left))  6.33 us
    ppermute x1, waiting for transfers between devices, shards(): over = lax.ppermute(over, 'gx', o_route)  6 us
    ppermute x1, starting transfers between devices, shards(): er = lax.ppermute(er, both, corner(e_route, to_right))  4.48 us
  transfers between devices with their start and end apart: 14, of which 6 were waited for; matrix products, arithmetic and copies ran while one was open for 16% of the time, Pallas kernels for 2%

profile of v1, /device:TPU:11, one launch (start us, length us, event | category | flops | bytes accessed | tf_op | source)
XLA Modules:
  0.0 132.6 jit_solution(15033748600612154564)
XLA Ops:
  0.0 3.1 %fusion.2 = (f32[4,512,128]{2,1,0:T(8,128)}, f32[4,512,128]{2,1,0:T(8,128)}) fusion(f32[4,512,512]{2,1,0:T(8,128)} %tile.1), kind=kLoop, calls=%fused_computation.19 | loop fusion | bytes 4194304 | tf_op jit(solution)/shard_map/slice | solution.py:386
  3.1 2.1 %collective-permute-start.1 = (f32[4,512,128]{2,1,0:T(8,128)}, f32[4,512,128]{2,1,0:T(8,128)S(1)}, u32[]{:S(2)}, u32[]{:S(2)}) collective-permute-start(f32[4,512,128]{2,1,0:T(8,128)} %get-tuple-element.29), channel_id=1, source_target_pairs={{1,0},{2,1},{3,2},{5,4},{6,5},{7,6},{9,8},{10,9},{11,10},{13,12},{... | collective-permute-start | bytes 3145736 | tf_op jit(solution)/shard_map/ppermute | solution.py:386
  5.1 3.2 %collective-permute-start = (f32[4,512,128]{2,1,0:T(8,128)}, f32[4,512,128]{2,1,0:T(8,128)S(1)}, u32[]{:S(2)}, u32[]{:S(2)}) collective-permute-start(f32[4,512,128]{2,1,0:T(8,128)} %get-tuple-element.30), channel_id=1, source_target_pairs={{0,1},{1,2},{2,3},{4,5},{5,6},{6,7},{8,9},{9,10},{10,11},{12,13},{... | collective-permute-start | bytes 3145736 | tf_op jit(solution)/shard_map/ppermute | solution.py:387
  8.4 2.8 %constant_dynamic-slice_fusion.1 = (f32[4,128,512]{2,1,0:T(8,128)S(1)}, f32[4,128,512]{2,1,0:T(8,128)}) fusion(f32[4,512,512]{2,1,0:T(8,128)} %tile.1, s32[]{:T(128)S(6)} %select_n.16, s32[]{:T(128)S(6)} %select_n.15), kind=kLoop, calls=%fused_computation.15 | loop fusion | bytes 4194312 | tf_op jit(solution)/shard_map/dynamic_slice | solution.py:375
  11.2 4.2 %collective-permute-start.2 = (f32[4,128,512]{2,1,0:T(8,128)}, f32[4,128,512]{2,1,0:T(8,128)S(1)}, u32[]{:S(2)}, u32[]{:S(2)}) collective-permute-start(f32[4,128,512]{2,1,0:T(8,128)} %get-tuple-element.28), channel_id=1, source_target_pairs={{4,8},{8,4},{12,16},{16,12},{20,24},{24,20},{5,9},{9,5},{13,17},{1... | collective-permute-start | bytes 3145736 | tf_op jit(solution)/shard_map/ppermute | solution.py:385
  15.4 13.8 %collective-permute-done.1.right = f32[4,512,128]{2,1,0:T(8,128)S(1)} collective-permute-done((f32[4,512,128]{2,1,0:T(8,128)}, f32[4,512,128]{2,1,0:T(8,128)S(1)}, u32[]{:S(2)}, u32[]{:S(2)}) %collective-permute-start.1) | collective-permute-done | bytes 1048608 | tf_op jit(solution)/shard_map/ppermute | solution.py:386
  29.2 1.8 %collective-permute-done.left = f32[4,512,128]{2,1,0:T(8,128)S(1)} collective-permute-done((f32[4,512,128]{2,1,0:T(8,128)}, f32[4,512,128]{2,1,0:T(8,128)S(1)}, u32[]{:S(2)}, u32[]{:S(2)}) %collective-permute-start) | collective-permute-done | bytes 1048608 | tf_op jit(solution)/shard_map/ppermute | solution.py:387
  31.0 1.2 pad_maximum_fusion
  32.3 1.8 %collective-permute-start.5 = (f32[4,128,768]{2,1,0:T(8,128)}, f32[4,128,768]{2,1,0:T(8,128)}, u32[]{:S(2)}, u32[]{:S(2)}) collective-permute-start(f32[4,128,768]{2,1,0:T(8,128)} %pad_maximum_fusion), channel_id=1, source_target_pairs={{0,4},{4,0},{8,12},{12,8},{16,20},{20,16},{24,28},{28,24},{1,5},{5... | collective-permute-start | bytes 4718600 | tf_op jit(solution)/shard_map/ppermute | solution.py:392
  36.8 2.2 %collective-permute-done.2.over = f32[4,128,512]{2,1,0:T(8,128)S(1)} collective-permute-done((f32[4,128,512]{2,1,0:T(8,128)}, f32[4,128,512]{2,1,0:T(8,128)S(1)}, u32[]{:S(2)}, u32[]{:S(2)}) %collective-permute-start.2) | collective-permute-done | bytes 1048608 | tf_op jit(solution)/shard_map/ppermute | solution.py:385
  39.9 2.1 %collective-permute-start.4 = (f32[4,128,128]{2,1,0:T(8,128)}, f32[4,128,128]{2,1,0:T(8,128)S(1)}, u32[]{:S(2)}, u32[]{:S(2)}) collective-permute-start(f32[4,128,128]{2,1,0:T(8,128)} %get-tuple-element.31), channel_id=1, source_target_pairs={{1,0},{2,1},{3,2},{5,4},{6,5},{7,6},{9,8},{10,9},{11,10},{13,12},{... | collective-permute-start | bytes 786440 | tf_op jit(solution)/shard_map/ppermute | solution.py:389
  42.0 3.3 %collective-permute-start.3 = (f32[4,128,128]{2,1,0:T(8,128)}, f32[4,128,128]{2,1,0:T(8,128)}, u32[]{:S(2)}, u32[]{:S(2)}) collective-permute-start(f32[4,128,128]{2,1,0:T(8,128)} %get-tuple-element.32), channel_id=1, source_target_pairs={{0,1},{1,2},{2,3},{4,5},{5,6},{6,7},{8,9},{9,10},{10,11},{12,13},{... | collective-permute-start | bytes 786440 | tf_op jit(solution)/shard_map/ppermute | solution.py:390
  45.3 3.2 %parity.1 = (f32[4,128,512]{2,1,0:T(8,128)}, f32[2,128,512]{2,1,0:T(8,128)}) custom-call(f32[4,256,256]{2,1,0:T(8,128)} %inten.1, f32[2,256,256]{2,1,0:T(8,128)} %pad_maximum_fusion.1.prop, bf16[256,256]{1,0:T(8,128)(2,1)} %constant.33.clone.pick), custom_call_target="tpu_custom_call" | custom-call | flops 4000000000 | bytes 3000000 | tf_op jit(solution)/shard_map/parity/pallas_call | solution.py:342
  49.1 2.3 %collective-permute-done.3.lcor = f32[4,128,128]{2,1,0:T(8,128)} collective-permute-done((f32[4,128,128]{2,1,0:T(8,128)}, f32[4,128,128]{2,1,0:T(8,128)}, u32[]{:S(2)}, u32[]{:S(2)}) %collective-permute-start.3) | collective-permute-done | bytes 262176 | tf_op jit(solution)/shard_map/ppermute | solution.py:390
  55.8 12.7 %frames.1 = (f32[4,512,512]{2,1,0:T(8,128)}, f32[4,512,128]{2,1,0:T(8,128)S(1)}, f32[4,512,128]{2,1,0:T(8,128)S(1)}, f32[4,128,512]{2,1,0:T(8,128)S(1)}, f32[4,1...) custom-call(s32[10]{0:T(128)S(1)} %pad_add_fusion.scal, ...), custom_call_target="tpu_custom_call" | custom-call | flops 40000000000 | bytes 30000000 | tf_op jit(solution)/shard_map/frames/pallas_call | solution.py:287
  68.4 12.9 %collective-permute-start.6 = (f32[4,128,512]{2,1,0:T(8,128)S(1)}, f32[4,128,512]{2,1,0:T(8,128)S(1)}, u32[]{:S(2)}, u32[]{:S(2)}) collective-permute-start(f32[4,128,512]{2,1,0:T(8,128)S(1)} %get-tuple-element.19), channel_id=1, source_target_pairs={{0,4},{4,0},{8,12},{12,8},{16,20},{20,16},{24,28},{28,24},{1,5},{5... | collective-permute-start | bytes 3145736 | tf_op jit(solution)/shard_map/ppermute | solution.py:406
  81.3 1.9 %collective-permute-start.7 = (f32[4,128,512]{2,1,0:T(8,128)S(1)}, f32[4,128,512]{2,1,0:T(8,128)S(1)}, u32[]{:S(2)}, u32[]{:S(2)}) collective-permute-start(f32[4,128,512]{2,1,0:T(8,128)S(1)} %get-tuple-element.20), channel_id=1, source_target_pairs={{4,8},{8,4},{12,16},{16,12},{20,24},{24,20},{5,9},{9,5},{13,17},{1... | collective-permute-start | bytes 3145736 | tf_op jit(solution)/shard_map/ppermute | solution.py:405
  83.3 7.8 %collective-permute-start.8 = (f32[4,512,128]{2,1,0:T(8,128)S(1)}, f32[4,512,128]{2,1,0:T(8,128)S(1)}, u32[]{:S(2)}, u32[]{:S(2)}) collective-permute-start(f32[4,512,128]{2,1,0:T(8,128)S(1)} %get-tuple-element.21), channel_id=1, source_target_pairs={{1,0},{2,1},{3,2},{5,4},{6,5},{7,6},{9,8},{10,9},{11,10},{13,12},{... | collective-permute-start | bytes 3145736 | tf_op jit(solution)/shard_map/ppermute | solution.py:403
  91.1 1.9 %collective-permute-start.9 = (f32[4,512,128]{2,1,0:T(8,128)S(1)}, f32[4,512,128]{2,1,0:T(8,128)S(1)}, u32[]{:S(2)}, u32[]{:S(2)}) collective-permute-start(f32[4,512,128]{2,1,0:T(8,128)S(1)} %get-tuple-element.22), channel_id=1, source_target_pairs={{0,1},{1,2},{2,3},{4,5},{5,6},{6,7},{8,9},{9,10},{10,11},{12,13},{... | collective-permute-start | bytes 3145736 | tf_op jit(solution)/shard_map/ppermute | solution.py:404
  93.0 6.3 %collective-permute-start.10 = (f32[4,128,128]{2,1,0:T(8,128)S(1)}, f32[4,128,128]{2,1,0:T(8,128)S(1)}, u32[]{:S(2)}, u32[]{:S(2)}) collective-permute-start(f32[4,128,128]{2,1,0:T(8,128)S(1)} %get-tuple-element.23), channel_id=1, source_target_pairs={{5,8},{6,9},{7,10},{9,4},{10,5},{11,6},{13,16},{14,17},{15,18},{17... | collective-permute-start | bytes 786440 | tf_op jit(solution)/shard_map/ppermute | solution.py:407
  99.4 3.2 %collective-permute-start.11 = (f32[4,128,128]{2,1,0:T(8,128)S(1)}, f32[4,128,128]{2,1,0:T(8,128)S(1)}, u32[]{:S(2)}, u32[]{:S(2)}) collective-permute-start(f32[4,128,128]{2,1,0:T(8,128)S(1)} %get-tuple-element.24), channel_id=1, source_target_pairs={{4,9},{5,10},{6,11},{8,5},{9,6},{10,7},{12,17},{13,18},{14,19},{16... | collective-permute-start | bytes 786440 | tf_op jit(solution)/shard_map/ppermute | solution.py:408
  102.6 2.4 %add_dynamic-update-slice_fusion.1 = f32[4,512,512]{2,1,0:T(8,128)} fusion(f32[4,512,512]{2,1,0:T(8,128)} %get-tuple-element.18, s32[]{:T(128)S(6)} %select_n.16, f32[4,128,512]{2,1,0:T(8,128)S(1)} %collective-permute-done.6), kind=kLoop, calls=%fused_computation.6 | loop fusion | flops 262144 | bytes 3145732 | tf_op jit(solution)/shard_map/dynamic_update_slice | solution.py:383
  105.0 6.0 %collective-permute-done.7 = f32[4,128,512]{2,1,0:T(8,128)S(1)} collective-permute-done((f32[4,128,512]{2,1,0:T(8,128)S(1)}, f32[4,128,512]{2,1,0:T(8,128)S(1)}, u32[]{:S(2)}, u32[]{:S(2)}) %collective-permute-start.7) | collective-permute-done | bytes 1048608 | tf_op jit(solution)/shard_map/ppermute | solution.py:405
  111.0 3.3 %collective-permute-start.12 = (f32[4,128,128]{2,1,0:T(8,128)S(1)}, f32[4,128,128]{2,1,0:T(8,128)S(1)}, u32[]{:S(2)}, u32[]{:S(2)}) collective-permute-start(f32[4,128,128]{2,1,0:T(8,128)S(1)} %get-tuple-element.25), channel_id=1, source_target_pairs={{1,4},{2,5},{3,6},{5,0},{6,1},{7,2},{9,12},{10,13},{11,14},{13,8},... | collective-permute-start | bytes 786440 | tf_op jit(solution)/shard_map/ppermute | solution.py:409
  114.3 2.4 %add_dynamic-update-slice_fusion = f32[4,512,512]{2,1,0:T(8,128)} fusion(f32[4,512,512]{2,1,0:T(8,128)} %add_dynamic-update-slice_fusion.1, s32[]{:T(128)S(6)} %select_n.15, f32[4,128,512]{2,1,0:T(8,128)S(1)} %collective-permute-done.7), kind=kLoop, calls=%fused_computation.5 | loop fusion | flops 262144 | bytes 3145732 | tf_op jit(solution)/shard_map/dynamic_update_slice | solution.py:383
  116.7 4.5 %collective-permute-start.13 = (f32[4,128,128]{2,1,0:T(8,128)S(1)}, f32[4,128,128]{2,1,0:T(8,128)S(1)}, u32[]{:S(2)}, u32[]{:S(2)}) collective-permute-start(f32[4,128,128]{2,1,0:T(8,128)S(1)} %get-tuple-element.26), channel_id=1, source_target_pairs={{0,5},{1,6},{2,7},{4,1},{5,2},{6,3},{8,13},{9,14},{10,15},{12,9},{... | collective-permute-start | bytes 786440 | tf_op jit(solution)/shard_map/ppermute | solution.py:410
  121.2 2.3 %fusion.1 = f32[4,512,512]{2,1,0:T(8,128)} fusion(f32[4,512,512]{2,1,0:T(8,128)} %add_dynamic-update-slice_fusion, f32[4,512,128]{2,1,0:T(8,128)S(1)} %collective-permute-done.8), kind=kLoop, calls=%fused_computation.4 | loop fusion | flops 262144 | bytes 3145728 | tf_op jit(solution)/shard_map/dynamic_update_slice | solution.py:383
  123.5 2.3 %fusion = f32[4,512,512]{2,1,0:T(8,128)} fusion(f32[4,512,512]{2,1,0:T(8,128)} %fusion.1, f32[4,512,128]{2,1,0:T(8,128)S(1)} %collective-permute-done.9), kind=kLoop, calls=%fused_computation.2 | loop fusion | flops 262144 | bytes 3145728 | tf_op jit(solution)/shard_map/dynamic_update_slice | solution.py:383
  125.8 1.7 %add_dynamic-update-slice_fusion.5 = f32[4,512,512]{2,1,0:T(8,128)} fusion(f32[4,512,512]{2,1,0:T(8,128)} %fusion, s32[]{:T(128)S(6)} %select_n.15, f32[4,128,128]{2,1,0:T(8,128)S(1)} %collective-permute-done.10), kind=kLoop, calls=%fused_computation.11 | loop fusion | flops 65536 | bytes 786436 | tf_op jit(solution)/shard_map/dynamic_update_slice | solution.py:383
  127.5 1.7 %add_dynamic-update-slice_fusion.4 = f32[4,512,512]{2,1,0:T(8,128)} fusion(f32[4,512,512]{2,1,0:T(8,128)} %add_dynamic-update-slice_fusion.5, s32[]{:T(128)S(6)} %select_n.15, f32[4,128,128]{2,1,0:T(8,128)S(1)} %collective-permute-done.11), kind=kLoop, calls=%fused_computation.10 | loop fusion | flops 65536 | bytes 786436 | tf_op jit(solution)/shard_map/dynamic_update_slice | solution.py:383
  129.2 1.7 %add_dynamic-update-slice_fusion.3 = f32[4,512,512]{2,1,0:T(8,128)} fusion(f32[4,512,512]{2,1,0:T(8,128)} %add_dynamic-update-slice_fusion.4, s32[]{:T(128)S(6)} %select_n.16, f32[4,128,128]{2,1,0:T(8,128)S(1)} %collective-permute-done.12), kind=kLoop, calls=%fused_computation.9 | loop fusion | flops 65536 | bytes 786436 | tf_op jit(solution)/shard_map/dynamic_update_slice | solution.py:383
  130.9 1.7 %add_dynamic-update-slice_fusion.2 = f32[4,512,512]{2,1,0:T(8,128)} fusion(f32[4,512,512]{2,1,0:T(8,128)} %add_dynamic-update-slice_fusion.3, s32[]{:T(128)S(6)} %select_n.16, f32[4,128,128]{2,1,0:T(8,128)S(1)} %collective-permute-done.13), kind=kLoop, calls=%fused_computation.8 | loop fusion | flops 65536 | bytes 786436 | tf_op jit(solution)/shard_map/dynamic_update_slice | solution.py:383
  (33 shorter events, 7.9 us)
Async XLA Ops:
  3.1 26.1 %collective-permute-start.1 = (f32[4,512,128]{2,1,0:T(8,128)}, f32[4,512,128]{2,1,0:T(8,128)S(1)}, u32[]{:S(2)}, u32[]{:S(2)}) collective-permute-start(f32[4,512,128]{2,1,0:T(8,128)} %get-tuple-element.29), channel_id=1, source_target_pairs={{1,0},{2,1},{3,2},{5,4},{6,5},{7,6},{9,8},{10,9},{11,10},{13,12},{... | collective-permute-start | bytes 3145736 | tf_op jit(solution)/shard_map/ppermute | solution.py:386
  5.1 25.9 %collective-permute-start = (f32[4,512,128]{2,1,0:T(8,128)}, f32[4,512,128]{2,1,0:T(8,128)S(1)}, u32[]{:S(2)}, u32[]{:S(2)}) collective-permute-start(f32[4,512,128]{2,1,0:T(8,128)} %get-tuple-element.30), channel_id=1, source_target_pairs={{0,1},{1,2},{2,3},{4,5},{5,6},{6,7},{8,9},{9,10},{10,11},{12,13},{... | collective-permute-start | bytes 3145736 | tf_op jit(solution)/shard_map/ppermute | solution.py:387
  8.4 26.4 %copy-start.7 = (s32[4,2]{0,1:T(2,128)S(1)}, s32[4,2]{0,1:T(2,128)}, u32[]{:S(2)}) copy-start(s32[4,2]{0,1:T(2,128)} %param.14) | copy-start | bytes 100
  8.4 26.6 %copy-start.6 = (f32[256,256]{1,0:T(8,128)S(1)}, f32[256,256]{1,0:T(8,128)}, u32[]{:S(2)}) copy-start(f32[256,256]{1,0:T(8,128)} %param.12) | copy-start | bytes 786436
  11.2 27.8 %collective-permute-start.2 = (f32[4,128,512]{2,1,0:T(8,128)}, f32[4,128,512]{2,1,0:T(8,128)S(1)}, u32[]{:S(2)}, u32[]{:S(2)}) collective-permute-start(f32[4,128,512]{2,1,0:T(8,128)} %get-tuple-element.28), channel_id=1, source_target_pairs={{4,8},{8,4},{12,16},{16,12},{20,24},{24,20},{5,9},{9,5},{13,17},{1... | collective-permute-start | bytes 3145736 | tf_op jit(solution)/shard_map/ppermute | solution.py:385
  32.3 19.1 %collective-permute-start.5 = (f32[4,128,768]{2,1,0:T(8,128)}, f32[4,128,768]{2,1,0:T(8,128)}, u32[]{:S(2)}, u32[]{:S(2)}) collective-permute-start(f32[4,128,768]{2,1,0:T(8,128)} %pad_maximum_fusion), channel_id=1, source_target_pairs={{0,4},{4,0},{8,12},{12,8},{16,20},{20,16},{24,28},{28,24},{1,5},{5... | collective-permute-start | bytes 4718600 | tf_op jit(solution)/shard_map/ppermute | solution.py:392
  39.9 9.2 %collective-permute-start.4 = (f32[4,128,128]{2,1,0:T(8,128)}, f32[4,128,128]{2,1,0:T(8,128)S(1)}, u32[]{:S(2)}, u32[]{:S(2)}) collective-permute-start(f32[4,128,128]{2,1,0:T(8,128)} %get-tuple-element.31), channel_id=1, source_target_pairs={{1,0},{2,1},{3,2},{5,4},{6,5},{7,6},{9,8},{10,9},{11,10},{13,12},{... | collective-permute-start | bytes 786440 | tf_op jit(solution)/shard_map/ppermute | solution.py:389
  42.0 9.4 %copy-start.2 = (f32[2,128,128]{2,1,0:T(8,128)S(1)}, f32[2,128,128]{2,1,0:T(8,128)}, u32[]{:S(2)}) copy-start(f32[2,128,128]{2,1,0:T(8,128)} %constant.36.clone.twc) | copy-start | bytes 393220
  42.0 9.4 %copy-start.3 = (f32[8,128]{1,0:T(8,128)S(1)}, f32[8,128]{1,0:T(8,128)}, u32[]{:S(2)}) copy-start(f32[8,128]{1,0:T(8,128)} %constant.35.clone.twl) | copy-start | bytes 12292
  42.0 9.4 %collective-permute-start.3 = (f32[4,128,128]{2,1,0:T(8,128)}, f32[4,128,128]{2,1,0:T(8,128)}, u32[]{:S(2)}, u32[]{:S(2)}) collective-permute-start(f32[4,128,128]{2,1,0:T(8,128)} %get-tuple-element.32), channel_id=1, source_target_pairs={{0,1},{1,2},{2,3},{4,5},{5,6},{6,7},{8,9},{9,10},{10,11},{12,13},{... | collective-permute-start | bytes 786440 | tf_op jit(solution)/shard_map/ppermute | solution.py:390
  51.4 1.0 copy-start
  52.4 1.0 copy-start.1
  53.5 1.2 copy-start.4
  54.7 1.0 copy-start.5
  68.4 30.9 %collective-permute-start.6 = (f32[4,128,512]{2,1,0:T(8,128)S(1)}, f32[4,128,512]{2,1,0:T(8,128)S(1)}, u32[]{:S(2)}, u32[]{:S(2)}) collective-permute-start(f32[4,128,512]{2,1,0:T(8,128)S(1)} %get-tuple-element.19), channel_id=1, source_target_pairs={{0,4},{4,0},{8,12},{12,8},{16,20},{20,16},{24,28},{28,24},{1,5},{5... | collective-permute-start | bytes 3145736 | tf_op jit(solution)/shard_map/ppermute | solution.py:406
  81.3 29.7 %collective-permute-start.7 = (f32[4,128,512]{2,1,0:T(8,128)S(1)}, f32[4,128,512]{2,1,0:T(8,128)S(1)}, u32[]{:S(2)}, u32[]{:S(2)}) collective-permute-start(f32[4,128,512]{2,1,0:T(8,128)S(1)} %get-tuple-element.20), channel_id=1, source_target_pairs={{4,8},{8,4},{12,16},{16,12},{20,24},{24,20},{5,9},{9,5},{13,17},{1... | collective-permute-start | bytes 3145736 | tf_op jit(solution)/shard_map/ppermute | solution.py:405
  83.3 33.5 %collective-permute-start.8 = (f32[4,512,128]{2,1,0:T(8,128)S(1)}, f32[4,512,128]{2,1,0:T(8,128)S(1)}, u32[]{:S(2)}, u32[]{:S(2)}) collective-permute-start(f32[4,512,128]{2,1,0:T(8,128)S(1)} %get-tuple-element.21), channel_id=1, source_target_pairs={{1,0},{2,1},{3,2},{5,4},{6,5},{7,6},{9,8},{10,9},{11,10},{13,12},{... | collective-permute-start | bytes 3145736 | tf_op jit(solution)/shard_map/ppermute | solution.py:403
  91.1 32.4 %collective-permute-start.9 = (f32[4,512,128]{2,1,0:T(8,128)S(1)}, f32[4,512,128]{2,1,0:T(8,128)S(1)}, u32[]{:S(2)}, u32[]{:S(2)}) collective-permute-start(f32[4,512,128]{2,1,0:T(8,128)S(1)} %get-tuple-element.22), channel_id=1, source_target_pairs={{0,1},{1,2},{2,3},{4,5},{5,6},{6,7},{8,9},{9,10},{10,11},{12,13},{... | collective-permute-start | bytes 3145736 | tf_op jit(solution)/shard_map/ppermute | solution.py:404
  93.0 32.8 %collective-permute-start.10 = (f32[4,128,128]{2,1,0:T(8,128)S(1)}, f32[4,128,128]{2,1,0:T(8,128)S(1)}, u32[]{:S(2)}, u32[]{:S(2)}) collective-permute-start(f32[4,128,128]{2,1,0:T(8,128)S(1)} %get-tuple-element.23), channel_id=1, source_target_pairs={{5,8},{6,9},{7,10},{9,4},{10,5},{11,6},{13,16},{14,17},{15,18},{17... | collective-permute-start | bytes 786440 | tf_op jit(solution)/shard_map/ppermute | solution.py:407
  99.4 28.2 %collective-permute-start.11 = (f32[4,128,128]{2,1,0:T(8,128)S(1)}, f32[4,128,128]{2,1,0:T(8,128)S(1)}, u32[]{:S(2)}, u32[]{:S(2)}) collective-permute-start(f32[4,128,128]{2,1,0:T(8,128)S(1)} %get-tuple-element.24), channel_id=1, source_target_pairs={{4,9},{5,10},{6,11},{8,5},{9,6},{10,7},{12,17},{13,18},{14,19},{16... | collective-permute-start | bytes 786440 | tf_op jit(solution)/shard_map/ppermute | solution.py:408
  111.0 18.2 %collective-permute-start.12 = (f32[4,128,128]{2,1,0:T(8,128)S(1)}, f32[4,128,128]{2,1,0:T(8,128)S(1)}, u32[]{:S(2)}, u32[]{:S(2)}) collective-permute-start(f32[4,128,128]{2,1,0:T(8,128)S(1)} %get-tuple-element.25), channel_id=1, source_target_pairs={{1,4},{2,5},{3,6},{5,0},{6,1},{7,2},{9,12},{10,13},{11,14},{13,8},... | collective-permute-start | bytes 786440 | tf_op jit(solution)/shard_map/ppermute | solution.py:409
  116.7 14.2 %collective-permute-start.13 = (f32[4,128,128]{2,1,0:T(8,128)S(1)}, f32[4,128,128]{2,1,0:T(8,128)S(1)}, u32[]{:S(2)}, u32[]{:S(2)}) collective-permute-start(f32[4,128,128]{2,1,0:T(8,128)S(1)} %get-tuple-element.26), channel_id=1, source_target_pairs={{0,5},{1,6},{2,7},{4,1},{5,2},{6,3},{8,13},{9,14},{10,15},{12,9},{... | collective-permute-start | bytes 786440 | tf_op jit(solution)/shard_map/ppermute | solution.py:410

commit v2 on v1

v2 whole, which is shorter than its diff:
```python
import math

import jax
import jax.numpy as jnp
import numpy as np
from jax import lax
from jax.experimental import pallas as pl
from jax.experimental.pallas import tpu as pltpu
from jax.sharding import PartitionSpec as P


ROWS = 32


def half_tables(frame):
    half = frame // 2
    n = np.arange(half)
    angle = 2.0 * np.pi * ((n[:, None] * n[None, :]) % half) / half
    scale = 1.0 / math.sqrt(frame)
    c, s = np.cos(angle) * scale, np.sin(angle) * scale
    right = np.block([[c, -s], [s, c]])
    turn = 2.0 * np.pi * n / frame
    return right, np.cos(turn), np.sin(turn)


def split_const(m):
    hi = m.astype(np.float32).astype(jnp.bfloat16)
    lo = (m - hi.astype(np.float64)).astype(np.float32).astype(jnp.bfloat16)
    return hi, lo


def mm(left, right):
    return jnp.dot(left, right, preferred_element_type=jnp.float32)


def cmul(ar, ai, br, bi):
    return ar * br - ai * bi, ar * bi + ai * br


def cmul_conj(ar, ai, br, bi):
    return ar * br + ai * bi, ar * bi - ai * br


def frame_kernel(
    scal, tile, left, right, over, oedge, ext_e, lcor, rcor, ecor, inten_in, probe_in, prop_in, mats_in, twl_in, twc_in,
    g_tile, g_lmain, g_rmain, g_ledge, g_redge, g_over, g_oedge, g_ext, g_ol, g_or,
    obj, acc, win, car, fld, lh, ll, rh, rl, dd, inten, probe, prop, mats, twl, twc, sems,
):
    frame = probe.shape[1]
    cap = inten.shape[0]
    half = frame // 2
    size = tile.shape[1]
    ntile = size // half
    even = scal[1] == 0
    e_row = jnp.where(even, half + size, 0)
    o_row = jnp.where(even, 0, half + size)
    e_row = pl.multiple_of(e_row, half)
    o_row = pl.multiple_of(o_row, half)
    mid = pl.ds(half, size)

    def blocks(array, width):
        return [array.at[:, :, pl.ds(half * j, half)] for j in range(width)]

    m_row = pl.multiple_of(jnp.where(even, half, frame), half)
    edge_row = pl.multiple_of(jnp.where(even, size, half), half)
    o_rows, e_rows = pl.ds(o_row, half), pl.ds(e_row, half)
    m_rows, edge_rows = pl.ds(m_row, size - half), pl.ds(edge_row, half)
    last = ntile + 1

    def moves(big, t, o, ol, orr, e):
        pairs = [(ol, big.at[:, 0, o_rows, :]), (orr, big.at[:, last, o_rows, :])]
        for j in range(ntile):
            pairs.append((o[j], big.at[:, j + 1, o_rows, :]))
            pairs.append((t[j], big.at[:, j + 1, mid, :]))
        for j in range(ntile + 2):
            pairs.append((e[j], big.at[:, j, e_rows, :]))
        return pairs

    def o_blocks(middle, ends):
        return [ends.at[0]] + blocks(middle, ntile - 2) + [ends.at[1]]

    routes = moves(
        obj, blocks(tile, ntile), o_blocks(over, oedge), lcor, rcor,
        [ecor.at[0]] + blocks(ext_e, ntile) + [ecor.at[1]],
    ) + [
        (left, obj.at[:, 0, mid, :]), (right, obj.at[:, last, mid, :]),
        (inten_in, inten), (probe_in, probe), (prop_in, prop), (mats_in, mats), (twl_in, twl), (twc_in, twc)
    ]
    loads = [pltpu.make_async_copy(src, dst, sems.at[i]) for i, (src, dst) in enumerate(routes)]
    for copy in loads:
        copy.start()

    def clear(i, carry):
        acc[i // (ntile + 2), i % (ntile + 2)] = jnp.zeros(acc.shape[2:], jnp.float32)
        return carry

    lax.fori_loop(0, acc.shape[0] * (ntile + 2), clear, 0)
    for copy in loads:
        copy.wait()

    lane = lax.broadcasted_iota(jnp.int32, (ROWS, half), 1)
    low, high = slice(0, half), slice(half, frame)

    def put(hi_ref, lo_ref, u, rows, cols, value):
        hi = value.astype(jnp.bfloat16)
        hi_ref[u, rows, cols] = hi
        lo_ref[u, rows, cols] = (value - hi.astype(jnp.float32)).astype(jnp.bfloat16)

    def right_product(u, m):
        dd[u] = mm(lh[u], mats[m]) + mm(ll[u], mats[m]) + mm(lh[u], mats[m + 1])

    def left_product(u, m):
        fld[u] = mm(mats[m], rh[u]) + mm(mats[m], rl[u]) + mm(mats[m + 1], rh[u])

    def right_forward(u, source):
        for rb in range(0, frame, ROWS):
            rows = slice(rb, rb + ROWS)
            xr, xi = source(u, rows)
            ar, br, ai, bi = xr[:, :half], xr[:, half:], xi[:, :half], xi[:, half:]
            put(lh, ll, u, rows, low, ar + br)
            put(lh, ll, u, rows, high, ai + bi)
            dr, di = ar - br, ai - bi
            c, s = twl[0:1, :], twl[1:2, :]
            vrows = slice(frame + rb, frame + rb + ROWS)
            put(lh, ll, u, vrows, low, dr * c + di * s)
            put(lh, ll, u, vrows, high, di * c - dr * s)
        right_product(u, 0)

    def left_forward(u):
        for q in range(2):
            for rb in range(0, half, ROWS):
                rows = slice(rb, rb + ROWS)
                t = slice(q * frame + rb, q * frame + rb + ROWS)
                b = slice(q * frame + half + rb, q * frame + half + rb + ROWS)
                ar, ai, br, bi = dd[u, t, low], dd[u, t, high], dd[u, b, low], dd[u, b, high]
                irows = slice(half + rb, half + rb + ROWS)
                ucols = slice(q * half, (q + 1) * half)
                vcols = slice(frame + q * half, frame + (q + 1) * half)
                put(rh, rl, u, rows, ucols, ar + br)
                put(rh, rl, u, irows, ucols, ai + bi)
                dr, di = ar - br, ai - bi
                c, s = twc[0, rows, :], twc[1, rows, :]
                put(rh, rl, u, rows, vcols, dr * c + di * s)
                put(rh, rl, u, irows, vcols, di * c - dr * s)
        left_product(u, 2)

    def left_inverse(u, source):
        for rb in range(0, half, ROWS):
            rows = slice(rb, rb + ROWS)
            xr, xi = source(u, rows)
            put(rh, rl, u, rows, slice(None), xr)
            put(rh, rl, u, slice(half + rb, half + rb + ROWS), slice(None), xi)
        left_product(u, 0)

    def right_inverse(u):
        for q in range(2):
            for rb in range(0, half, ROWS):
                rows = slice(rb, rb + ROWS)
                irows = slice(half + rb, half + rb + ROWS)
                ecols = slice(q * half, (q + 1) * half)
                ocols = slice(frame + q * half, frame + (q + 1) * half)
                er, ei = fld[u, rows, ecols], fld[u, irows, ecols]
                wr, wi = fld[u, rows, ocols], fld[u, irows, ocols]
                c, s = twc[0, rows, :], twc[1, rows, :]
                tr, ti = wr * c - wi * s, wi * c + wr * s
                top = slice(q * frame + rb, q * frame + rb + ROWS)
                bot = slice(q * frame + half + rb, q * frame + half + rb + ROWS)
                put(lh, ll, u, top, low, er + tr)
                put(lh, ll, u, top, high, ei + ti)
                put(lh, ll, u, bot, low, er - tr)
                put(lh, ll, u, bot, high, ei - ti)
        right_product(u, 2)

    def finish(u, sink):
        for rb in range(0, frame, ROWS):
            rows = slice(rb, rb + ROWS)
            orows = slice(frame + rb, frame + rb + ROWS)
            er, ei, wr, wi = dd[u, rows, low], dd[u, rows, high], dd[u, orows, low], dd[u, orows, high]
            c, s = twl[0:1, :], twl[1:2, :]
            tr, ti = wr * c - wi * s, wi * c + wr * s
            sink(u, rows, er + tr, ei + ti, er - tr, ei - ti)

    def step(i, carry):
        first = 2 * i
        slots = (first, jnp.minimum(first + 1, cap - 1))
        live = (None, first + 1 < scal[0])
        spots = []
        for slot in slots:
            r, c = scal[2 + 2 * slot], scal[3 + 2 * slot]
            j = jnp.minimum(c // half, ntile - 1)
            cs = c - j * half
            spots.append((r, j, cs, lax.rem(half - cs, half), lax.rem(cs, half)))

        def load(u, k):
            r, j, cs, back, _ = spots[u]
            keep = lane + cs < half
            for rb in range(0, frame, ROWS):
                parts = [
                    pltpu.roll(obj[k, j + t, pl.ds(r + rb, ROWS), :], back, 1) for t in range(3)
                ]
                win[u, k, rb:rb + ROWS, low] = jnp.where(keep, parts[0], parts[1])
                win[u, k, rb:rb + ROWS, high] = jnp.where(keep, parts[1], parts[2])

        def place(u, k, rows, first, second):
            r, j, cs, _, fore = spots[u]
            zero = jnp.zeros_like(first)
            if live[u] is not None:
                first = jnp.where(live[u], first, zero)
                second = jnp.where(live[u], second, zero)
            spill = lane >= cs
            a, b = pltpu.roll(first, fore, 1), pltpu.roll(second, fore, 1)
            at = pl.ds(r + rows.start, ROWS)
            acc[k, j, at, :] += jnp.where(spill, a, zero)
            acc[k, j + 1, at, :] += jnp.where(spill, b, a)
            acc[k, j + 2, at, :] += jnp.where(spill, zero, b)

        def lower(rows):
            return slice(half + rows.start, half + rows.stop)

        def enter(u, rows):
            return cmul(probe[0, rows, :], probe[1, rows, :], win[u, 0, rows, :], win[u, 1, rows, :])

        def propagate(u, rows):
            return cmul(prop[0, rows, :], prop[1, rows, :], fld[u, rows, :], fld[u, lower(rows), :])

        def propagate_back(u, rows):
            return cmul_conj(prop[0, rows, :], prop[1, rows, :], fld[u, rows, :], fld[u, lower(rows), :])

        def carried(u, rows, ar, ai, br, bi):
            car[u, 0, rows, low] = ar
            car[u, 1, rows, low] = ai
            car[u, 0, rows, high] = br
            car[u, 1, rows, high] = bi

        def exit_wave(u, rows):
            return cmul(car[u, 0, rows, :], car[u, 1, rows, :], win[u, 2, rows, :], win[u, 3, rows, :])

        def misfit(u, rows):
            fr, fi = fld[u, rows, :], fld[u, lower(rows), :]
            m = fr * fr + fi * fi - inten[slots[u], rows, :]
            return m * fr, m * fi

        def grad_exit(u, rows, ar, ai, br, bi):
            lr, li = cmul_conj(car[u, 0, rows, low], car[u, 1, rows, low], ar, ai)
            hr, hi = cmul_conj(car[u, 0, rows, high], car[u, 1, rows, high], br, bi)
            place(u, 2, rows, lr, hr)
            place(u, 3, rows, li, hi)
            for cols, (gr, gi) in ((low, (ar, ai)), (high, (br, bi))):
                xr, xi = cmul_conj(win[u, 2, rows, cols], win[u, 3, rows, cols], gr, gi)
                win[u, 0, rows, cols] = xr
                win[u, 1, rows, cols] = xi

        def inner(u, rows):
            return win[u, 0, rows, :], win[u, 1, rows, :]

        def grad_enter(u, rows, ar, ai, br, bi):
            lr, li = cmul_conj(probe[0, rows, low], probe[1, rows, low], ar, ai)
            hr, hi = cmul_conj(probe[0, rows, high], probe[1, rows, high], br, bi)
            place(u, 0, rows, lr, hr)
            place(u, 1, rows, li, hi)

        both = (0, 1)
        phases = [
            lambda u: [load(u, 0), load(u, 1), right_forward(u, enter)],
            left_forward,
            lambda u: left_inverse(u, propagate),
            right_inverse,
            lambda u: [finish(u, carried), load(u, 2), load(u, 3), right_forward(u, exit_wave)],
            left_forward,
            lambda u: left_inverse(u, misfit),
            right_inverse,
            lambda u: [finish(u, grad_exit), right_forward(u, inner)],
            left_forward,
            lambda u: left_inverse(u, propagate_back),
            right_inverse,
            lambda u: finish(u, grad_enter),
        ]
        for phase in phases:
            for u in both:
                phase(u)
        return carry

    lax.fori_loop(0, (scal[0] + 1) // 2, step, 0)

    targets = moves(
        acc, blocks(g_tile, ntile), o_blocks(g_over, g_oedge), g_ol, g_or, blocks(g_ext, ntile + 2)
    ) + [
        (g_lmain, acc.at[:, 0, m_rows, :]), (g_rmain, acc.at[:, last, m_rows, :]),
        (g_ledge, acc.at[:, 0, edge_rows, :]), (g_redge, acc.at[:, last, edge_rows, :]),
    ]
    stores = [pltpu.make_async_copy(src, dst, sems.at[i]) for i, (dst, src) in enumerate(targets)]
    for copy in stores:
        copy.start()
    for copy in stores:
        copy.wait()


def run_frames(scal, pieces, inten, probe, prop, frame):
    right, tc, ts = half_tables(frame)
    half = frame // 2
    rhi, rlo = split_const(right)
    mats = np.stack([rhi, rlo, np.ascontiguousarray(rhi.T), np.ascontiguousarray(rlo.T)])
    twl = np.zeros((8, half), np.float32)
    twl[0], twl[1] = tc, ts
    twc = np.stack([np.repeat(tc[:, None], half, 1), np.repeat(ts[:, None], half, 1)]).astype(np.float32)
    channels, size, _ = pieces[0].shape
    ntile = size // half
    hbm = pl.BlockSpec(memory_space=pl.ANY)
    vmem = pl.BlockSpec(memory_space=pltpu.VMEM)
    big = (channels, ntile + 2, size + frame, half)
    tile, _, _, over, oedge, _, cor = pieces[:7]
    main = (channels, size - half, half)
    strip = (channels, half, size + frame)
    outs = [
        jax.ShapeDtypeStruct(shape, jnp.float32)
        for shape in (
            tile.shape, main, main, cor.shape, cor.shape, over.shape, oedge.shape, strip, cor.shape, cor.shape
        )
    ]
    operands = (inten, probe, prop, mats, twl, twc)
    copies = 3 * ntile + 8 + len(operands)
    return pl.pallas_call(
        frame_kernel,
        out_shape=outs,
        in_specs=[pl.BlockSpec(memory_space=pltpu.SMEM)] + [hbm] * len(pieces) + [pl.BlockSpec(memory_space=pltpu.HBM)] * len(operands),
        out_specs=[hbm] * len(outs),
        scratch_shapes=[
            pltpu.VMEM(big, jnp.float32),
            pltpu.VMEM(big, jnp.float32),
            pltpu.VMEM((2, 4, frame, frame), jnp.float32),
            pltpu.VMEM((2, 2, frame, frame), jnp.float32),
            pltpu.VMEM((2, frame, 2 * frame), jnp.float32),
            pltpu.VMEM((2, 2 * frame, frame), jnp.bfloat16),
            pltpu.VMEM((2, 2 * frame, frame), jnp.bfloat16),
            pltpu.VMEM((2, frame, 2 * frame), jnp.bfloat16),
            pltpu.VMEM((2, frame, 2 * frame), jnp.bfloat16),
            pltpu.VMEM((2, 2 * frame, frame), jnp.float32),
        ]
        + [pltpu.VMEM(x.shape, x.dtype) for x in operands]
        + [pltpu.SemaphoreType.DMA((copies,))],
        compiler_params=pltpu.CompilerParams(vmem_limit_bytes=36 * 1024 * 1024),
        cost_estimate=pl.CostEstimate(flops=40_000_000_000, bytes_accessed=30_000_000, transcendentals=0),
        name="frames",
    )(scal, *pieces, *operands)


def merge_kernel(scal, tile, right, left, redge, ledge, over, oedge, ext, out, stage, sems):
    channels, size, _ = stage.shape
    w = right.shape[2]
    even = scal[1] == 0
    far = size - w
    e_row = pl.multiple_of(jnp.where(even, far, 0), w)
    o_row = pl.multiple_of(jnp.where(even, 0, far), w)
    m_row = pl.multiple_of(jnp.where(even, 0, w), w)
    lo, mid, hi = slice(0, w), slice(w, far), slice(far, size)
    e_rows, o_rows, m_rows = pl.ds(e_row, w), pl.ds(o_row, w), pl.ds(m_row, far)
    copies = []
    for k in range(channels):
        stage[k] = tile[k]
        stage[k, m_rows, hi] += right[k]
        stage[k, m_rows, lo] += left[k]
        stage[k, o_rows, mid] += over[k]
        stage[k, o_rows, lo] += oedge[0, k]
        stage[k, o_rows, hi] += oedge[1, k]
        stage[k, e_rows, :] += ext[k, :, w:-w]
        stage[k, e_rows, hi] += redge[k]
        stage[k, e_rows, lo] += ledge[k]
        copy = pltpu.make_async_copy(stage.at[k], out.at[k], sems.at[k])
        copy.start()
        copies.append(copy)
    for copy in copies:
        copy.wait()


def merge(scal, tile, *parts):
    vmem = pl.BlockSpec(memory_space=pltpu.VMEM)
    return pl.pallas_call(
        merge_kernel,
        out_shape=jax.ShapeDtypeStruct(tile.shape, jnp.float32),
        in_specs=[pl.BlockSpec(memory_space=pltpu.SMEM)] + [vmem] * (1 + len(parts)),
        out_specs=pl.BlockSpec(memory_space=pl.ANY),
        scratch_shapes=[
            pltpu.VMEM(tile.shape, jnp.float32),
            pltpu.SemaphoreType.DMA((tile.shape[0],)),
        ],
        compiler_params=pltpu.CompilerParams(vmem_limit_bytes=20 * 1024 * 1024),
        cost_estimate=pl.CostEstimate(flops=10_000_000, bytes_accessed=13_000_000, transcendentals=0),
        name="merge",
    )(scal, tile, *parts)


def parity_kernel(inten, prop, pick, inten_out, prop_out, mid):
    half = pick.shape[0] // 2

    def sort(src, dst, index):
        x = src[index]
        top = x.astype(jnp.bfloat16)
        rest = x - top.astype(jnp.float32)
        middle = rest.astype(jnp.bfloat16)
        last = (rest - middle.astype(jnp.float32)).astype(jnp.bfloat16)
        out = mm(top, pick[...]) + mm(middle, pick[...]) + mm(last, pick[...])
        mid[2 * index] = out[:, :half]
        mid[2 * index + 1] = out[:, half:]
        for q in range(2):
            for p in range(2):
                cols = slice((2 * q + p) * half, (2 * q + p + 1) * half)
                dst[index, :, cols] = mid[2 * index + p, pl.ds(q, half, stride=2), :]

    for i in range(inten.shape[0]):
        sort(inten, inten_out, i)
    for i in range(prop.shape[0]):
        sort(prop, prop_out, i)


def by_parity(inten, prop):
    frame = inten.shape[-1]
    half = frame // 2
    pick = np.zeros((frame, frame), np.float32)
    n = np.arange(half)
    pick[2 * n, n] = 1.0
    pick[2 * n + 1, half + n] = 1.0
    vmem = pl.BlockSpec(memory_space=pltpu.VMEM)
    return pl.pallas_call(
        parity_kernel,
        out_shape=[
            jax.ShapeDtypeStruct((x.shape[0], half, 2 * frame), jnp.float32) for x in (inten, prop)
        ],
        in_specs=[vmem] * 3,
        out_specs=[vmem] * 2,
        scratch_shapes=[pltpu.VMEM((2 * inten.shape[0], frame, half), jnp.float32)],
        compiler_params=pltpu.CompilerParams(vmem_limit_bytes=12 * 1024 * 1024),
        cost_estimate=pl.CostEstimate(flops=4_000_000_000, bytes_accessed=3_000_000, transcendentals=0),
        name="parity",
    )(inten, prop, pick.astype(jnp.bfloat16))


def pair_route(count, first):
    route = []
    for i in range(first, count - 1, 2):
        route += [(i, i + 1), (i + 1, i)]
    return route


def shards(objects, probe_wave, prop_phase, intensity, offsets, counts):
    frame = intensity.shape[1]
    margin = frame // 2
    size_r, _ = objects.shape[1:]
    nx, ny = lax.axis_size("gx"), lax.axis_size("gy")
    parity = lax.axis_index("gx") % 2
    to_left = [(i, i - 1) for i in range(1, ny)]
    to_right = [(i, i + 1) for i in range(ny - 1)]
    e_route, o_route = pair_route(nx, 0), pair_route(nx, 1)
    e_start = jnp.where(parity == 0, size_r - margin, 0)
    o_start = jnp.where(parity == 0, 0, size_r - margin)

    def band(x, start):
        return lax.dynamic_slice_in_dim(x, start, margin, 1)

    o_band = band(objects, o_start)
    ends = jnp.stack([o_band[:, :, :margin], o_band[:, :, -margin:]])
    oedge = lax.ppermute(ends, "gx", o_route)
    right = lax.ppermute(objects[:, :, :margin], "gy", to_left)
    left = lax.ppermute(objects[:, :, -margin:], "gy", to_right)
    over = lax.ppermute(o_band[:, :, margin:-margin], "gx", o_route)
    first, last = oedge[0], oedge[1]
    rcor = lax.ppermute(first, "gy", to_left)
    lcor = lax.ppermute(last, "gy", to_right)

    waves = jnp.stack([jnp.cos(prop_phase), jnp.sin(prop_phase)])
    inten, waves = by_parity(intensity, waves)
    later, inten = lax.optimization_barrier((objects, inten))
    ext = lax.ppermute(band(later, e_start), "gx", e_route)
    ecor = lax.ppermute(jnp.stack([band(left, e_start), band(right, e_start)]), "gx", e_route)

    scal = jnp.concatenate([counts, parity[None].astype(jnp.int32), offsets.reshape(-1)])
    pieces = [objects, left, right, over, oedge, ext, lcor, rcor, ecor]
    tile, left, right, ledge, redge, over, oedge, ext, ol, orr = run_frames(
        scal, pieces, inten, probe_wave, waves, frame
    )

    ext = lax.ppermute(ext, "gx", e_route)
    ol = lax.ppermute(ol, "gy", to_left)
    orr = lax.ppermute(orr, "gy", to_right)
    left = lax.ppermute(left, "gy", to_left)
    right = lax.ppermute(right, "gy", to_right)
    over = lax.ppermute(over, "gx", o_route)
    ledge = ledge + ext[:, :, :margin]
    redge = redge + ext[:, :, -margin:]
    oedge = oedge + jnp.stack([orr, ol])
    ledge = lax.ppermute(ledge, "gy", to_left)
    redge = lax.ppermute(redge, "gy", to_right)
    oedge = lax.ppermute(oedge, "gx", o_route)
    return merge(scal, tile, left, right, ledge, redge, over, oedge, ext)


def solution(mesh):
    return jax.shard_map(
        shards,
        mesh=mesh,
        in_specs=(
            P(None, "gx", "gy"),
            P(),
            P(),
            P(("gx", "gy"), None, None),
            P(("gx", "gy"), None),
            P(("gx", "gy")),
        ),
        out_specs=P(None, "gx", "gy"),
        check_vma=False,
    )
```

time: 135 us -> 113 us (0.84); the launches traced: 133 us -> 112 us
  other arithmetic: 18.3 us -> 1.91 us
  starting transfers between devices: 58.6 us -> 50.1 us
  local copies, waits for them, and re-layouts: 12.2 us -> 16.8 us
    dynamic_update_slice x8 -> x0, other arithmetic: 16.2 us -> none  [add_at(): return lax.dynamic_update_slice(x, old + update, at)]
    ppermute x8 -> x11, waiting for transfers between devices: 2.25 us -> 15.5 us  [the longest x1 9.32 us: shards(): oedge = lax.ppermute(oedge, 'gx', o_route)]
    ppermute x1, waiting for transfers between devices: 13.8 us -> 2.13 us  [shards(): right = lax.ppermute(objects[:, :, :margin], 'gy', to_left)]
    ppermute x1, starting transfers between devices: 12.9 us -> 6.28 us  [shards(): ext = lax.ppermute(ext, 'gx', e_route)]
    pallas_call x0 -> x1, Pallas kernels: none -> 2.78 us  [merge(): pl.pallas_call(merge_kernel, out_shape=jax.ShapeDtypeStruct(tile.shape, j...]
    pallas_call x1, Pallas kernels: 3.22 us -> 0.89 us  [by_parity(): pl.pallas_call(parity_kernel, out_shape=[jax.ShapeDtypeStruct((x.shape[0]...]
    unnamed x17 -> x25, local copies, waits for them, and re-layouts: 4.46 us -> 6.43 us
    ppermute x1, waiting for transfers between devices: 2.29 us -> 0.44 us  [shards(): lcor = lax.ppermute(last, 'gy', to_right)]
  transfers between devices with their start and end apart: 14 -> 17, of which waited for: 6 -> 8; matrix products, arithmetic and copies ran while one was open for 16% -> 8% of each run, Pallas kernels for 2% -> 1%
where the time goes in v2:
time: 113 us; the launch traced here: 112 us
  starting transfers between devices  50.1 us (44%)
  waiting for transfers between devices  26.2 us (23%)
  local copies, waits for them, and re-layouts  16.8 us (15%)
  Pallas kernels  16.1 us (14%)
  other arithmetic  1.91 us (2%)
    pallas_call x1, Pallas kernels, run_frames(): pl.pallas_call(frame_kernel, out_shape=outs, in_specs=[pl.BlockSpec(memor...  12.4 us
    ppermute x1, waiting for transfers between devices, shards(): oedge = lax.ppermute(oedge, 'gx', o_route)  9.32 us
    unnamed x25, local copies, waits for them, and re-layouts  6.43 us
    ppermute x1, waiting for transfers between devices, shards(): over = lax.ppermute(over, 'gx', o_route)  6.41 us
    ppermute x1, starting transfers between devices, shards(): ext = lax.ppermute(ext, 'gx', e_route)  6.28 us
    ppermute x1, starting transfers between devices, shards(): oedge = lax.ppermute(oedge, 'gx', o_route)  4.45 us
    ppermute x1, starting transfers between devices, shards(): right = lax.ppermute(right, 'gy', to_right)  4.2 us
    ppermute x1, starting transfers between devices, shards(): orr = lax.ppermute(orr, 'gy', to_right)  4.14 us
  transfers between devices with their start and end apart: 17, of which 8 were waited for; matrix products, arithmetic and copies ran while one was open for 8% of the time, Pallas kernels for 1%

profile of v2, /device:TPU:11, one launch (start us, length us, event | category | flops | bytes accessed | tf_op | source)
XLA Modules:
  0.0 112.0 jit_solution(4054913378007773360)
XLA Ops:
  0.0 3.1 %fusion = (f32[4,512,128]{2,1,0:T(8,128)}, f32[4,512,128]{2,1,0:T(8,128)}) fusion(f32[4,512,512]{2,1,0:T(8,128)} %tile.1), kind=kLoop, calls=%fused_computation.17 | loop fusion | bytes 4194304 | tf_op jit(solution)/shard_map/slice | solution.py:462
  3.1 2.1 %collective-permute-start.1 = (f32[4,512,128]{2,1,0:T(8,128)}, f32[4,512,128]{2,1,0:T(8,128)S(1)}, u32[]{:S(2)}, u32[]{:S(2)}) collective-permute-start(f32[4,512,128]{2,1,0:T(8,128)} %get-tuple-element.35), channel_id=1, source_target_pairs={{1,0},{2,1},{3,2},{5,4},{6,5},{7,6},{9,8},{10,9},{11,10},{13,12},{... | collective-permute-start | bytes 3145736 | tf_op jit(solution)/shard_map/ppermute | solution.py:462
  5.2 3.2 %collective-permute-start = (f32[4,512,128]{2,1,0:T(8,128)}, f32[4,512,128]{2,1,0:T(8,128)S(1)}, u32[]{:S(2)}, u32[]{:S(2)}) collective-permute-start(f32[4,512,128]{2,1,0:T(8,128)} %get-tuple-element.36), channel_id=1, source_target_pairs={{0,1},{1,2},{2,3},{4,5},{5,6},{6,7},{8,9},{9,10},{10,11},{12,13},{... | collective-permute-start | bytes 3145736 | tf_op jit(solution)/shard_map/ppermute | solution.py:463
  9.4 1.2 %copy-done = f32[4,256,256]{2,1,0:T(8,128)S(1)} copy-done((f32[4,256,256]{2,1,0:T(8,128)S(1)}, f32[4,256,256]{2,1,0:T(8,128)}, u32[]{:S(2)}) %copy-start) | copy-done | bytes 1048600
  13.4 2.4 %constant_dynamic-slice_fusion.1 = f32[4,128,512]{2,1,0:T(8,128)} fusion(f32[4,512,512]{2,1,0:T(8,128)} %tile.1, s32[]{:T(128)S(6)} %select_n.20), kind=kLoop, calls=%fused_computation.15 | loop fusion | bytes 2097156 | tf_op jit(solution)/shard_map/dynamic_slice | solution.py:457
  15.7 1.2 %collective-permute-start.4 = (f32[4,128,512]{2,1,0:T(8,128)}, f32[4,128,512]{2,1,0:T(8,128)}, u32[]{:S(2)}, u32[]{:S(2)}) collective-permute-start(f32[4,128,512]{2,1,0:T(8,128)} %constant_dynamic-slice_fusion.1), channel_id=1, source_target_pairs={{0,4},{4,0},{8,12},{12,8},{16,20},{20,16},{24,28},{28,24},{1,5},{5... | collective-permute-start | bytes 3145736 | tf_op jit(solution)/shard_map/ppermute | solution.py:472
  16.9 1.1 dynamic-slice_bitcast_fusion.1
  18.9 3.0 %collective-permute-start.3 = (f32[2,4,128,128]{3,2,1,0:T(8,128)}, f32[2,4,128,128]{3,2,1,0:T(8,128)S(1)}, u32[]{:S(2)}, u32[]{:S(2)}) collective-permute-start(f32[2,4,128,128]{3,2,1,0:T(8,128)} %pad_maximum_fusion), channel_id=1, source_target_pairs={{4,8},{8,4},{12,16},{16,12},{20,24},{24,20},{5,9},{9,5},{13,17},{1... | collective-permute-start | bytes 1572872 | tf_op jit(solution)/shard_map/ppermute | solution.py:461
  21.9 1.9 %constant_dynamic-slice_fusion = f32[4,128,256]{2,1,0:T(8,128)} fusion(f32[4,512,512]{2,1,0:T(8,128)} %tile.1, s32[]{:T(128)S(6)} %select_n.19, s32[]{:T(128)S(6)} %add.23), kind=kLoop, calls=%fused_computation.14 | loop fusion | bytes 1048584 | tf_op jit(solution)/shard_map/slice | solution.py:464
  23.7 3.4 %collective-permute-start.2 = (f32[4,128,256]{2,1,0:T(8,128)}, f32[4,128,256]{2,1,0:T(8,128)}, u32[]{:S(2)}, u32[]{:S(2)}) collective-permute-start(f32[4,128,256]{2,1,0:T(8,128)} %constant_dynamic-slice_fusion), channel_id=1, source_target_pairs={{4,8},{8,4},{12,16},{16,12},{20,24},{24,20},{5,9},{9,5},{13,17},{1... | collective-permute-start | bytes 1572872 | tf_op jit(solution)/shard_map/ppermute | solution.py:464
  27.2 2.1 %collective-permute-done.1.right = f32[4,512,128]{2,1,0:T(8,128)S(1)} collective-permute-done((f32[4,512,128]{2,1,0:T(8,128)}, f32[4,512,128]{2,1,0:T(8,128)S(1)}, u32[]{:S(2)}, u32[]{:S(2)}) %collective-permute-start.1) | collective-permute-done | bytes 1048608 | tf_op jit(solution)/shard_map/ppermute | solution.py:462
  29.3 1.8 %collective-permute-done.left = f32[4,512,128]{2,1,0:T(8,128)S(1)} collective-permute-done((f32[4,512,128]{2,1,0:T(8,128)}, f32[4,512,128]{2,1,0:T(8,128)S(1)}, u32[]{:S(2)}, u32[]{:S(2)}) %collective-permute-start) | collective-permute-done | bytes 1048608 | tf_op jit(solution)/shard_map/ppermute | solution.py:463
  32.0 1.7 %collective-permute-start.7 = (f32[2,4,128,128]{3,2,1,0:T(8,128)}, f32[2,4,128,128]{3,2,1,0:T(8,128)}, u32[]{:S(2)}, u32[]{:S(2)}) collective-permute-start(f32[2,4,128,128]{3,2,1,0:T(8,128)} %pad_maximum_fusion.2), channel_id=1, source_target_pairs={{0,4},{4,0},{8,12},{12,8},{16,20},{20,16},{24,28},{28,24},{1,5},{5... | collective-permute-start | bytes 1572872 | tf_op jit(solution)/shard_map/ppermute | solution.py:473
  33.7 2.4 %collective-permute-done.3.oedge = f32[2,4,128,128]{3,2,1,0:T(8,128)S(1)} collective-permute-done((f32[2,4,128,128]{3,2,1,0:T(8,128)}, f32[2,4,128,128]{3,2,1,0:T(8,128)S(1)}, u32[]{:S(2)}, u32[]{:S(2)}) %collective-permute-start.3) | collective-permute-done | bytes 524320 | tf_op jit(solution)/shard_map/ppermute | solution.py:461
  36.9 2.1 %collective-permute-start.6 = (f32[4,128,128]{2,1,0:T(8,128)}, f32[4,128,128]{2,1,0:T(8,128)S(1)}, u32[]{:S(2)}, u32[]{:S(2)}) collective-permute-start(f32[4,128,128]{2,1,0:T(8,128)} %get-tuple-element.39), channel_id=1, source_target_pairs={{1,0},{2,1},{3,2},{5,4},{6,5},{7,6},{9,8},{10,9},{11,10},{13,12},{... | collective-permute-start | bytes 786440 | tf_op jit(solution)/shard_map/ppermute | solution.py:466
  39.1 3.1 %collective-permute-start.5 = (f32[4,128,128]{2,1,0:T(8,128)}, f32[4,128,128]{2,1,0:T(8,128)}, u32[]{:S(2)}, u32[]{:S(2)}) collective-permute-start(f32[4,128,128]{2,1,0:T(8,128)} %get-tuple-element.40), channel_id=1, source_target_pairs={{0,1},{1,2},{2,3},{4,5},{5,6},{6,7},{8,9},{9,10},{10,11},{12,13},{... | collective-permute-start | bytes 786440 | tf_op jit(solution)/shard_map/ppermute | solution.py:467
  43.1 3.7 %collective-permute-done.2.over = f32[4,128,256]{2,1,0:T(8,128)} collective-permute-done((f32[4,128,256]{2,1,0:T(8,128)}, f32[4,128,256]{2,1,0:T(8,128)}, u32[]{:S(2)}, u32[]{:S(2)}) %collective-permute-start.2) | collective-permute-done | bytes 524320 | tf_op jit(solution)/shard_map/ppermute | solution.py:464
  48.3 1.2 %copy-done.7 = f32[4,128,512]{2,1,0:T(8,128)S(1)} copy-done((f32[4,128,512]{2,1,0:T(8,128)S(1)}, f32[4,128,512]{2,1,0:T(8,128)}, u32[]{:S(2)}) %copy-start.7) | copy-done | bytes 1048600
  49.5 1.0 copy-done.9
  50.6 12.4 %frames.1 = (f32[4,512,512]{2,1,0:T(8,128)S(1)}, f32[4,384,128]{2,1,0:T(8,128)S(1)}, f32[4,384,128]{2,1,0:T(8,128)S(1)}, f32[4,128,128]{2,1,0:T(8,128)S(1)}, f32...) custom-call(s32[10]{0:T(128)S(1)} %pad_add_fusion.scal, ...), custom_call_target="tpu_custom_call" | custom-call | flops 40000000000 | bytes 30000000 | tf_op jit(solution)/shard_map/frames/pallas_call | solution.py:322
  63.0 6.3 %collective-permute-start.10 = (f32[4,128,768]{2,1,0:T(8,128)S(1)}, f32[4,128,768]{2,1,0:T(8,128)S(1)}, u32[]{:S(2)}, u32[]{:S(2)}) collective-permute-start(f32[4,128,768]{2,1,0:T(8,128)S(1)} %get-tuple-element.27), channel_id=1, source_target_pairs={{0,4},{4,0},{8,12},{12,8},{16,20},{20,16},{24,28},{28,24},{1,5},{5... | collective-permute-start | bytes 4718600 | tf_op jit(solution)/shard_map/ppermute | solution.py:481
  69.3 4.1 %collective-permute-start.14 = (f32[4,128,128]{2,1,0:T(8,128)S(1)}, f32[4,128,128]{2,1,0:T(8,128)S(1)}, u32[]{:S(2)}, u32[]{:S(2)}) collective-permute-start(f32[4,128,128]{2,1,0:T(8,128)S(1)} %get-tuple-element.31), channel_id=1, source_target_pairs={{0,1},{1,2},{2,3},{4,5},{5,6},{6,7},{8,9},{9,10},{10,11},{12,13},{... | collective-permute-start | bytes 786440 | tf_op jit(solution)/shard_map/ppermute | solution.py:483
  73.4 1.9 %collective-permute-start.15 = (f32[4,128,128]{2,1,0:T(8,128)S(1)}, f32[4,128,128]{2,1,0:T(8,128)S(1)}, u32[]{:S(2)}, u32[]{:S(2)}) collective-permute-start(f32[4,128,128]{2,1,0:T(8,128)S(1)} %get-tuple-element.32), channel_id=1, source_target_pairs={{1,0},{2,1},{3,2},{5,4},{6,5},{7,6},{9,8},{10,9},{11,10},{13,12},{... | collective-permute-start | bytes 786440 | tf_op jit(solution)/shard_map/ppermute | solution.py:482
  75.3 1.9 %collective-permute-start.8 = (f32[4,384,128]{2,1,0:T(8,128)S(1)}, f32[4,384,128]{2,1,0:T(8,128)S(1)}, u32[]{:S(2)}, u32[]{:S(2)}) collective-permute-start(f32[4,384,128]{2,1,0:T(8,128)S(1)} %get-tuple-element.24), channel_id=1, source_target_pairs={{1,0},{2,1},{3,2},{5,4},{6,5},{7,6},{9,8},{10,9},{11,10},{13,12},{... | collective-permute-start | bytes 2359304 | tf_op jit(solution)/shard_map/ppermute | solution.py:484
  77.3 4.2 %collective-permute-start.9 = (f32[4,384,128]{2,1,0:T(8,128)S(1)}, f32[4,384,128]{2,1,0:T(8,128)S(1)}, u32[]{:S(2)}, u32[]{:S(2)}) collective-permute-start(f32[4,384,128]{2,1,0:T(8,128)S(1)} %get-tuple-element.25), channel_id=1, source_target_pairs={{0,1},{1,2},{2,3},{4,5},{5,6},{6,7},{8,9},{9,10},{10,11},{12,13},{... | collective-permute-start | bytes 2359304 | tf_op jit(solution)/shard_map/ppermute | solution.py:485
  81.5 1.9 %collective-permute-start.13 = (f32[4,128,256]{2,1,0:T(8,128)S(1)}, f32[4,128,256]{2,1,0:T(8,128)S(1)}, u32[]{:S(2)}, u32[]{:S(2)}) collective-permute-start(f32[4,128,256]{2,1,0:T(8,128)S(1)} %get-tuple-element.29), channel_id=1, source_target_pairs={{4,8},{8,4},{12,16},{16,12},{20,24},{24,20},{5,9},{9,5},{13,17},{1... | collective-permute-start | bytes 1572872 | tf_op jit(solution)/shard_map/ppermute | solution.py:486
  83.6 4.5 %collective-permute-start.16 = (f32[2,4,128,128]{3,2,1,0:T(8,128)S(1)}, f32[2,4,128,128]{3,2,1,0:T(8,128)S(1)}, u32[]{:S(2)}, u32[]{:S(2)}) collective-permute-start(f32[2,4,128,128]{3,2,1,0:T(8,128)S(1)} %maximum_add_fusion), channel_id=1, source_target_pairs={{4,8},{8,4},{12,16},{16,12},{20,24},{24,20},{5,9},{9,5},{13,17},{1... | collective-permute-start | bytes 1572872 | tf_op jit(solution)/shard_map/ppermute | solution.py:492
  88.1 3.4 %collective-permute-start.12 = (f32[4,128,128]{2,1,0:T(8,128)S(1)}, f32[4,128,128]{2,1,0:T(8,128)S(1)}, u32[]{:S(2)}, u32[]{:S(2)}) collective-permute-start(f32[4,128,128]{2,1,0:T(8,128)S(1)} %get-tuple-element.37), channel_id=1, source_target_pairs={{0,1},{1,2},{2,3},{4,5},{5,6},{6,7},{8,9},{9,10},{10,11},{12,13},{... | collective-permute-start | bytes 786440 | tf_op jit(solution)/shard_map/ppermute | solution.py:491
  91.5 6.4 %collective-permute-done.13.over = f32[4,128,256]{2,1,0:T(8,128)S(1)} collective-permute-done((f32[4,128,256]{2,1,0:T(8,128)S(1)}, f32[4,128,256]{2,1,0:T(8,128)S(1)}, u32[]{:S(2)}, u32[]{:S(2)}) %collective-permute-start.13) | collective-permute-done | bytes 524320 | tf_op jit(solution)/shard_map/ppermute | solution.py:486
  98.0 1.9 %collective-permute-start.11 = (f32[4,128,128]{2,1,0:T(8,128)S(1)}, f32[4,128,128]{2,1,0:T(8,128)S(1)}, u32[]{:S(2)}, u32[]{:S(2)}) collective-permute-start(f32[4,128,128]{2,1,0:T(8,128)S(1)} %get-tuple-element.38), channel_id=1, source_target_pairs={{1,0},{2,1},{3,2},{5,4},{6,5},{7,6},{9,8},{10,9},{11,10},{13,12},{... | collective-permute-start | bytes 786440 | tf_op jit(solution)/shard_map/ppermute | solution.py:490
  99.9 9.3 %collective-permute-done.16.oedge = f32[2,4,128,128]{3,2,1,0:T(8,128)S(1)} collective-permute-done((f32[2,4,128,128]{3,2,1,0:T(8,128)S(1)}, f32[2,4,128,128]{3,2,1,0:T(8,128)S(1)}, u32[]{:S(2)}, u32[]{:S(2)}) %collective-permute-start.16) | collective-permute-done | bytes 524320 | tf_op jit(solution)/shard_map/ppermute | solution.py:492
  109.2 2.8 %merge.1 = f32[4,512,512]{2,1,0:T(8,128)} custom-call(s32[10]{0:T(128)S(1)} %pad_add_fusion.scal, f32[4,512,512]{2,1,0:T(8,128)S(1)} %get-tuple-element.23.tile, f32[4,384,128]{2,1,0:T(8,128)S(1)} %collective-permute-done.8.right, f32[4,384,128]{2,1,0:T(8,128)S(1)} %collective-permute-done.9.left, f32[4,128,128]{2,1,0:T(8,128)S(1)} %collective-permute-done.11.redge, ...), custom_call_target="tpu_custom_call" | custom-call | flops 10000000 | bytes 13000000 | tf_op jit(solution)/shard_map/merge/pallas_call | solution.py:377
  (45 shorter events, 8.3 us)
Async XLA Ops:
  0.0 9.4 %copy-start.4 = (bf16[256,256]{1,0:T(8,128)(2,1)S(1)}, bf16[256,256]{1,0:T(8,128)(2,1)}, u32[]{:S(2)}) copy-start(bf16[256,256]{1,0:T(8,128)(2,1)} %constant.33.clone.pick) | copy-start | bytes 393220
  0.0 8.4 %copy-start.10 = (f32[256,256]{1,0:T(8,128)S(1)}, f32[256,256]{1,0:T(8,128)}, u32[]{:S(2)}) copy-start(f32[256,256]{1,0:T(8,128)} %param.12) | copy-start | bytes 786436
  3.1 26.2 %collective-permute-start.1 = (f32[4,512,128]{2,1,0:T(8,128)}, f32[4,512,128]{2,1,0:T(8,128)S(1)}, u32[]{:S(2)}, u32[]{:S(2)}) collective-permute-start(f32[4,512,128]{2,1,0:T(8,128)} %get-tuple-element.35), channel_id=1, source_target_pairs={{1,0},{2,1},{3,2},{5,4},{6,5},{7,6},{9,8},{10,9},{11,10},{13,12},{... | collective-permute-start | bytes 3145736 | tf_op jit(solution)/shard_map/ppermute | solution.py:462
  5.2 26.0 %collective-permute-start = (f32[4,512,128]{2,1,0:T(8,128)}, f32[4,512,128]{2,1,0:T(8,128)S(1)}, u32[]{:S(2)}, u32[]{:S(2)}) collective-permute-start(f32[4,512,128]{2,1,0:T(8,128)} %get-tuple-element.36), channel_id=1, source_target_pairs={{0,1},{1,2},{2,3},{4,5},{5,6},{6,7},{8,9},{9,10},{10,11},{12,13},{... | collective-permute-start | bytes 3145736 | tf_op jit(solution)/shard_map/ppermute | solution.py:463
  9.4 1.2 %copy-start = (f32[4,256,256]{2,1,0:T(8,128)S(1)}, f32[4,256,256]{2,1,0:T(8,128)}, u32[]{:S(2)}) copy-start(f32[4,256,256]{2,1,0:T(8,128)} %inten.1) | copy-start | bytes 3145732
  11.5 1.0 copy-start.6
  12.5 0.8 copy-start.8
  13.4 29.5 %copy-start.11 = (s32[4,2]{0,1:T(2,128)S(1)}, s32[4,2]{0,1:T(2,128)}, u32[]{:S(2)}) copy-start(s32[4,2]{0,1:T(2,128)} %param.14) | copy-start | bytes 100
  13.4 33.9 %copy-start.1 = (f32[2,256,256]{2,1,0:T(8,128)S(1)}, f32[2,256,256]{2,1,0:T(8,128)}, u32[]{:S(2)}) copy-start(f32[2,256,256]{2,1,0:T(8,128)} %probe_in.1) | copy-start | bytes 1572868
  13.4 33.9 %copy-start.3 = (f32[2,128,128]{2,1,0:T(8,128)S(1)}, f32[2,128,128]{2,1,0:T(8,128)}, u32[]{:S(2)}) copy-start(f32[2,128,128]{2,1,0:T(8,128)} %constant.36.clone.twc_in) | copy-start | bytes 393220
  13.4 33.9 %copy-start.5 = (f32[8,128]{1,0:T(8,128)S(1)}, f32[8,128]{1,0:T(8,128)}, u32[]{:S(2)}) copy-start(f32[8,128]{1,0:T(8,128)} %constant.35.clone.twl_in) | copy-start | bytes 12292
  15.7 31.5 %collective-permute-start.4 = (f32[4,128,512]{2,1,0:T(8,128)}, f32[4,128,512]{2,1,0:T(8,128)}, u32[]{:S(2)}, u32[]{:S(2)}) collective-permute-start(f32[4,128,512]{2,1,0:T(8,128)} %constant_dynamic-slice_fusion.1), channel_id=1, source_target_pairs={{0,4},{4,0},{8,12},{12,8},{16,20},{20,16},{24,28},{28,24},{1,5},{5... | collective-permute-start | bytes 3145736 | tf_op jit(solution)/shard_map/ppermute | solution.py:472
  18.9 17.2 %collective-permute-start.3 = (f32[2,4,128,128]{3,2,1,0:T(8,128)}, f32[2,4,128,128]{3,2,1,0:T(8,128)S(1)}, u32[]{:S(2)}, u32[]{:S(2)}) collective-permute-start(f32[2,4,128,128]{3,2,1,0:T(8,128)} %pad_maximum_fusion), channel_id=1, source_target_pairs={{4,8},{8,4},{12,16},{16,12},{20,24},{24,20},{5,9},{9,5},{13,17},{1... | collective-permute-start | bytes 1572872 | tf_op jit(solution)/shard_map/ppermute | solution.py:461
  23.7 23.0 %collective-permute-start.2 = (f32[4,128,256]{2,1,0:T(8,128)}, f32[4,128,256]{2,1,0:T(8,128)}, u32[]{:S(2)}, u32[]{:S(2)}) collective-permute-start(f32[4,128,256]{2,1,0:T(8,128)} %constant_dynamic-slice_fusion), channel_id=1, source_target_pairs={{4,8},{8,4},{12,16},{16,12},{20,24},{24,20},{5,9},{9,5},{13,17},{1... | collective-permute-start | bytes 1572872 | tf_op jit(solution)/shard_map/ppermute | solution.py:464
  32.0 15.2 %collective-permute-start.7 = (f32[2,4,128,128]{3,2,1,0:T(8,128)}, f32[2,4,128,128]{3,2,1,0:T(8,128)}, u32[]{:S(2)}, u32[]{:S(2)}) collective-permute-start(f32[2,4,128,128]{3,2,1,0:T(8,128)} %pad_maximum_fusion.2), channel_id=1, source_target_pairs={{0,4},{4,0},{8,12},{12,8},{16,20},{20,16},{24,28},{28,24},{1,5},{5... | collective-permute-start | bytes 1572872 | tf_op jit(solution)/shard_map/ppermute | solution.py:473
  36.9 9.9 %collective-permute-start.6 = (f32[4,128,128]{2,1,0:T(8,128)}, f32[4,128,128]{2,1,0:T(8,128)S(1)}, u32[]{:S(2)}, u32[]{:S(2)}) collective-permute-start(f32[4,128,128]{2,1,0:T(8,128)} %get-tuple-element.39), channel_id=1, source_target_pairs={{1,0},{2,1},{3,2},{5,4},{6,5},{7,6},{9,8},{10,9},{11,10},{13,12},{... | collective-permute-start | bytes 786440 | tf_op jit(solution)/shard_map/ppermute | solution.py:466
  39.1 8.2 %collective-permute-start.5 = (f32[4,128,128]{2,1,0:T(8,128)}, f32[4,128,128]{2,1,0:T(8,128)}, u32[]{:S(2)}, u32[]{:S(2)}) collective-permute-start(f32[4,128,128]{2,1,0:T(8,128)} %get-tuple-element.40), channel_id=1, source_target_pairs={{0,1},{1,2},{2,3},{4,5},{5,6},{6,7},{8,9},{9,10},{10,11},{12,13},{... | collective-permute-start | bytes 786440 | tf_op jit(solution)/shard_map/ppermute | solution.py:467
  47.3 1.0 copy-start.2
  48.3 1.2 %copy-start.7 = (f32[4,128,512]{2,1,0:T(8,128)S(1)}, f32[4,128,512]{2,1,0:T(8,128)}, u32[]{:S(2)}) copy-start(f32[4,128,512]{2,1,0:T(8,128)} %copy-done.6) | copy-start | bytes 3145732
  49.5 1.0 copy-start.9
  63.0 25.1 %collective-permute-start.10 = (f32[4,128,768]{2,1,0:T(8,128)S(1)}, f32[4,128,768]{2,1,0:T(8,128)S(1)}, u32[]{:S(2)}, u32[]{:S(2)}) collective-permute-start(f32[4,128,768]{2,1,0:T(8,128)S(1)} %get-tuple-element.27), channel_id=1, source_target_pairs={{0,4},{4,0},{8,12},{12,8},{16,20},{20,16},{24,28},{28,24},{1,5},{5... | collective-permute-start | bytes 4718600 | tf_op jit(solution)/shard_map/ppermute | solution.py:481
  69.3 12.2 %collective-permute-start.14 = (f32[4,128,128]{2,1,0:T(8,128)S(1)}, f32[4,128,128]{2,1,0:T(8,128)S(1)}, u32[]{:S(2)}, u32[]{:S(2)}) collective-permute-start(f32[4,128,128]{2,1,0:T(8,128)S(1)} %get-tuple-element.31), channel_id=1, source_target_pairs={{0,1},{1,2},{2,3},{4,5},{5,6},{6,7},{8,9},{9,10},{10,11},{12,13},{... | collective-permute-start | bytes 786440 | tf_op jit(solution)/shard_map/ppermute | solution.py:483
  73.4 10.1 %collective-permute-start.15 = (f32[4,128,128]{2,1,0:T(8,128)S(1)}, f32[4,128,128]{2,1,0:T(8,128)S(1)}, u32[]{:S(2)}, u32[]{:S(2)}) collective-permute-start(f32[4,128,128]{2,1,0:T(8,128)S(1)} %get-tuple-element.32), channel_id=1, source_target_pairs={{1,0},{2,1},{3,2},{5,4},{6,5},{7,6},{9,8},{10,9},{11,10},{13,12},{... | collective-permute-start | bytes 786440 | tf_op jit(solution)/shard_map/ppermute | solution.py:482
  75.3 33.9 %collective-permute-start.8 = (f32[4,384,128]{2,1,0:T(8,128)S(1)}, f32[4,384,128]{2,1,0:T(8,128)S(1)}, u32[]{:S(2)}, u32[]{:S(2)}) collective-permute-start(f32[4,384,128]{2,1,0:T(8,128)S(1)} %get-tuple-element.24), channel_id=1, source_target_pairs={{1,0},{2,1},{3,2},{5,4},{6,5},{7,6},{9,8},{10,9},{11,10},{13,12},{... | collective-permute-start | bytes 2359304 | tf_op jit(solution)/shard_map/ppermute | solution.py:484
  77.3 31.9 %collective-permute-start.9 = (f32[4,384,128]{2,1,0:T(8,128)S(1)}, f32[4,384,128]{2,1,0:T(8,128)S(1)}, u32[]{:S(2)}, u32[]{:S(2)}) collective-permute-start(f32[4,384,128]{2,1,0:T(8,128)S(1)} %get-tuple-element.25), channel_id=1, source_target_pairs={{0,1},{1,2},{2,3},{4,5},{5,6},{6,7},{8,9},{9,10},{10,11},{12,13},{... | collective-permute-start | bytes 2359304 | tf_op jit(solution)/shard_map/ppermute | solution.py:485
  81.5 16.5 %collective-permute-start.13 = (f32[4,128,256]{2,1,0:T(8,128)S(1)}, f32[4,128,256]{2,1,0:T(8,128)S(1)}, u32[]{:S(2)}, u32[]{:S(2)}) collective-permute-start(f32[4,128,256]{2,1,0:T(8,128)S(1)} %get-tuple-element.29), channel_id=1, source_target_pairs={{4,8},{8,4},{12,16},{16,12},{20,24},{24,20},{5,9},{9,5},{13,17},{1... | collective-permute-start | bytes 1572872 | tf_op jit(solution)/shard_map/ppermute | solution.py:486
  83.6 25.6 %collective-permute-start.16 = (f32[2,4,128,128]{3,2,1,0:T(8,128)S(1)}, f32[2,4,128,128]{3,2,1,0:T(8,128)S(1)}, u32[]{:S(2)}, u32[]{:S(2)}) collective-permute-start(f32[2,4,128,128]{3,2,1,0:T(8,128)S(1)} %maximum_add_fusion), channel_id=1, source_target_pairs={{4,8},{8,4},{12,16},{16,12},{20,24},{24,20},{5,9},{9,5},{13,17},{1... | collective-permute-start | bytes 1572872 | tf_op jit(solution)/shard_map/ppermute | solution.py:492
  88.1 21.1 %collective-permute-start.12 = (f32[4,128,128]{2,1,0:T(8,128)S(1)}, f32[4,128,128]{2,1,0:T(8,128)S(1)}, u32[]{:S(2)}, u32[]{:S(2)}) collective-permute-start(f32[4,128,128]{2,1,0:T(8,128)S(1)} %get-tuple-element.37), channel_id=1, source_target_pairs={{0,1},{1,2},{2,3},{4,5},{5,6},{6,7},{8,9},{9,10},{10,11},{12,13},{... | collective-permute-start | bytes 786440 | tf_op jit(solution)/shard_map/ppermute | solution.py:491
  98.0 11.3 %collective-permute-start.11 = (f32[4,128,128]{2,1,0:T(8,128)S(1)}, f32[4,128,128]{2,1,0:T(8,128)S(1)}, u32[]{:S(2)}, u32[]{:S(2)}) collective-permute-start(f32[4,128,128]{2,1,0:T(8,128)S(1)} %get-tuple-element.38), channel_id=1, source_target_pairs={{1,0},{2,1},{3,2},{5,4},{6,5},{7,6},{9,8},{10,9},{11,10},{13,12},{... | collective-permute-start | bytes 786440 | tf_op jit(solution)/shard_map/ppermute | solution.py:490
